TPU v7x, 256 devices: a whole 4x4x8 slice. The times are simulated.
256 devices in a mesh: grp: 4 (over x), dev: 64 (over y, z, core).
Axes of the slice: x: 4, y: 4, z: 8, core: 2. Of those that a mesh axis runs over, the one named last changes fastest.
Arguments:
- obs_coord: float32 [3, 1048576], P(None, ('grp', 'dev')), may hold values from -1 to 1
- obs_resid: float32 [1048576], P(('grp', 'dev')), may hold values from -6 to 6
- obs_weight: float32 [1048576], P(('grp', 'dev')), may hold values from 0.5 to 2
- obs_dest: int32 [1048576], P(('grp', 'dev')), may hold values from 0 to 63, as said below
- obs_send_slot: int32 [1048576], P(('grp', 'dev')), may hold values from 0 to 127, as said below
- obs_elem: int32 [1048576], P(('grp', 'dev')), may hold values from 0 to 255, as said below
- obs_slot: int32 [1048576], P(('grp', 'dev')), may hold values from 0 to 31, as said below
Outputs:
- nodal: float32 [16, 512, 8, 512], P('grp', 'dev')
- total_cost: float32 [], replicated
Inputs may be any that keep to these rules, and one draw needn't show every extreme that they name: `obs_dest`: from the rows of one device, at most 128 observations go to any one destination; in every group one destination receives exactly 128 from every device of the group. `obs_send_slot`: distinct among the rows of one device with the same obs_dest. `obs_elem`: together with obs_slot distinct among all observations of a group with the same obs_dest. `obs_slot`: on every destination some element uses all 32 slots.
All inputs are finite; a program needn't handle non-finite values.
Results may differ from a plain program's by a relative error of at most 0.00017.
Values sent between devices are 32-bit elements; how exact they have to be, the bound alone decides.
A program may use at most 64 MiB of HBM per device.

v0:
```python
import functools
import math

import jax
import jax.numpy as jnp
from jax import lax
from jax.sharding import Mesh
from jax.sharding import PartitionSpec as P

EX = 4
EY = 8
EZ = 8
ELEM_DEV = 256
SLOTS = 32
DEV = ("dev_0", "dev_1", "dev_2")
GRP_DEV = ("grp", "dev_0", "dev_1", "dev_2")


def by_axis(array, axes):
    return functools.reduce(lax.psum, axes, array)


def with_halo(block, sides, width):
    for axis, dim in sides:
        count = lax.axis_size(axis)
        forward = [(i, i + 1) for i in range(count - 1)]
        backward = [(target, source) for source, target in forward]
        low = lax.ppermute(
            lax.slice_in_dim(block, block.shape[dim] - width, None, axis=dim), axis, forward
        )
        high = lax.ppermute(lax.slice_in_dim(block, 0, width, axis=dim), axis, backward)
        block = jnp.concatenate([low, block, high], axis=dim)
    return block


def basis_values(position):
    anchors = [-math.cos(math.pi * k / 7) for k in range(8)]
    basis = []
    for node_i in range(8):
        factor = jnp.ones_like(position)
        for node_m in range(8):
            if node_m != node_i:
                factor = factor * (
                    (position - anchors[node_m]) / (anchors[node_i] - anchors[node_m])
                )
        basis.append(factor)
    return jnp.stack(basis)


def contract(first_w, second_w, third_w):
    outer = (first_w[:, None, :] * second_w[None, :, :]).reshape(64, ELEM_DEV, SLOTS)
    third = third_w.reshape(8, ELEM_DEV, SLOTS)
    mixed = jnp.einsum("aes,kes->eak", outer, third, precision=lax.Precision.HIGHEST)
    return mixed.reshape(ELEM_DEV, 512)


def combine(field, elem_dim, node_dim, from_low, from_high):
    count = field.shape[elem_dim]
    low_plane = lax.slice_in_dim(field, 0, 1, axis=node_dim)
    high_plane = lax.slice_in_dim(field, 7, 8, axis=node_dim)
    after = jnp.concatenate(
        [lax.slice_in_dim(low_plane, 1, count, axis=elem_dim), from_high], axis=elem_dim
    )
    before = jnp.concatenate(
        [from_low, lax.slice_in_dim(high_plane, 0, count - 1, axis=elem_dim)], axis=elem_dim
    )
    middle = lax.slice_in_dim(field, 1, 7, axis=node_dim)
    return jnp.concatenate([low_plane + before, middle, high_plane + after], axis=node_dim)


def boundary(field, elem_dim, node_dim):
    count = field.shape[elem_dim]
    low_plane = lax.slice_in_dim(field, 0, 1, axis=node_dim)
    high_plane = lax.slice_in_dim(field, 7, 8, axis=node_dim)
    return jnp.concatenate(
        [
            lax.slice_in_dim(low_plane, 0, 1, axis=elem_dim),
            lax.slice_in_dim(high_plane, count - 1, count, axis=elem_dim),
        ],
        axis=elem_dim,
    )


def on_device(obs_coord, obs_resid, obs_weight, obs_dest, obs_send_slot, obs_elem, obs_slot):
    peer_count = lax.axis_size(DEV)
    row_count = obs_resid.shape[0]
    capacity = 2 * row_count // peer_count
    cell_count = ELEM_DEV * SLOTS
    forcing = obs_weight * obs_resid
    total_cost = by_axis(0.5 * jnp.sum(forcing * obs_resid), GRP_DEV)
    payload = jnp.concatenate([obs_coord, forcing[None, :]], axis=0)
    channels = payload.shape[0]
    target = obs_dest * capacity + obs_send_slot
    cell_ids = obs_elem * SLOTS + obs_slot
    send_values = (
        jnp.zeros((channels, peer_count * capacity), payload.dtype).at[:, target].set(payload)
    )
    send_cells = jnp.full((peer_count * capacity,), cell_count, jnp.int32).at[target].set(cell_ids)
    send_values = send_values.reshape(channels, peer_count, capacity)
    send_cells = send_cells.reshape(1, peer_count, capacity)
    got_values, got_cells = (
        lax.all_to_all(send_values, DEV, split_axis=1, concat_axis=1, tiled=True),
        lax.all_to_all(send_cells, DEV, split_axis=1, concat_axis=1, tiled=True),
    )
    packed = jnp.zeros((channels, cell_count + 1), payload.dtype)
    packed = packed.at[:, got_cells.reshape(-1)].set(got_values.reshape(channels, -1))[
        :, :cell_count
    ]
    first_w = basis_values(packed[0]) * packed[3]
    second_w = basis_values(packed[1])
    third_w = basis_values(packed[2])
    field = contract(first_w, second_w, third_w).reshape(EX, EY, EZ, 8, 8, 8)
    padded = with_halo(boundary(field, 0, 3), (("grp", 0),), 1)
    field = combine(field, 0, 3, padded[0:1], padded[3:4])
    padded = with_halo(boundary(field, 1, 4), ((DEV, 1),), 1)
    field = combine(field, 1, 4, padded[:, 0:1], padded[:, 3:4])
    empty = jnp.zeros_like(lax.slice_in_dim(lax.slice_in_dim(field, 0, 1, axis=5), 0, 1, axis=2))
    field = combine(field, 2, 5, empty, empty)
    return (field.reshape(EX, EY, EZ, 512), total_cost)


def solution(mesh):
    torus = Mesh(
        mesh.devices.reshape(mesh.shape["grp"], 4, 8, 2), ("grp", "dev_0", "dev_1", "dev_2")
    )
    placed = (
        P(None, GRP_DEV),
        P(GRP_DEV),
        P(GRP_DEV),
        P(GRP_DEV),
        P(GRP_DEV),
        P(GRP_DEV),
        P(GRP_DEV),
    )
    return jax.shard_map(
        on_device,
        mesh=torus,
        in_specs=placed,
        out_specs=(P("grp", DEV, None, None), P()),
        check_vma=False,
    )
```

profile of v0, /device:TPU:1, one launch (start us, length us, event | category | flops | bytes accessed | tf_op | source)
XLA Modules:
  0.0 236.1 jit_solution(15072114107615707539)
XLA Ops:
  0.6 1.3 multiply_reduce_fusion.8
  2.6 9.8 %psum.28 = f32[]{:T(128)} all-reduce(f32[]{:T(128)S(6)} %mul_shard_map.3), channel_id=1, replica_groups=mesh['grp'=4,'dev_0'=4,'dev_1'=8,'dev_2'=2] {'grp'}, use_global_device_ids=true, to_apply=%region_4.0 | all-reduce | flops 1 | bytes 8 | tf_op jit(solution)/shard_map/psum | solution.py:20
  12.4 9.6 %psum.29 = f32[]{:T(128)} all-reduce(f32[]{:T(128)} %psum.28), channel_id=1, replica_groups=mesh['grp'=4,'dev_0'=4,'dev_1'=8,'dev_2'=2] {'dev_0'}, use_global_device_ids=true, to_apply=%region_5.0 | all-reduce | flops 1 | bytes 8 | tf_op jit(solution)/shard_map/psum | solution.py:20
  22.8 16.1 %scatter_custom_fusion = s32[8192]{0:T(1024)} fusion(s32[4096]{0:T(1024)S(1)} %get-tuple-element.54, s32[4096]{0:T(1024)S(1)} %get-tuple-element.55, s32[]{:T(128)} %constant.245.clone.1), kind=kCustom, calls=%fused_computation.88 | custom fusion | bytes 32772 | tf_op jit(solution)/shard_map/scatter | solution.py:98
  38.9 13.8 %all-to-all-start = ((s32[1,64,128]{2,0,1:T(1,128)}), s32[1,64,128]{2,0,1:T(1,128)S(1)}, u32[]{:S(2)}, u32[]{:S(2)}) async-start(s32[1,64,128]{2,0,1:T(1,128)} %bitcast), calls=%async_computation | async-start | bytes 65536 | tf_op jit(solution)/shard_map/all_to_all | solution.py:103
  52.6 14.5 %psum.30 = f32[]{:T(128)} all-reduce(f32[]{:T(128)} %psum.29), channel_id=1, replica_groups=mesh['grp'=4,'dev_0'=4,'dev_1'=8,'dev_2'=2] {'dev_1'}, use_global_device_ids=true, to_apply=%region_6.0 | all-reduce | flops 1 | bytes 8 | tf_op jit(solution)/shard_map/psum | solution.py:20
  68.0 6.3 %psum.31 = f32[]{:T(128)} all-reduce(f32[]{:T(128)} %psum.30), channel_id=1, replica_groups=mesh['grp'=4,'dev_0'=4,'dev_1'=8,'dev_2'=2] {'dev_2'}, use_global_device_ids=true, to_apply=%region_7.0 | all-reduce | flops 1 | bytes 8 | tf_op jit(solution)/shard_map/psum | solution.py:20
  75.0 12.8 %scatter_custom_fusion.1 = f32[4,8192]{0,1:T(8,128)} fusion(s32[4096]{0:T(1024)S(1)} %get-tuple-element.54, f32[4096,4]{1,0:T(8,128)S(1)} %copy.404, f32[]{:T(128)} %constant.244.clone.1), kind=kCustom, calls=%fused_computation.11 | custom fusion | bytes 131076 | tf_op jit(solution)/shard_map/scatter | solution.py:96
  87.7 3.5 %copy.405 = f32[4,64,128]{2,0,1:T(4,128)} copy(f32[4,64,128]{0,2,1:T(8,128)} %bitcast.27) | data formatting | bytes 262144 | tf_op jit(solution)/shard_map/reshape | solution.py:99
  91.2 8.0 %all-to-all-start.1 = ((f32[4,64,128]{2,0,1:T(4,128)}), f32[4,64,128]{2,0,1:T(4,128)S(1)}, u32[]{:S(2)}, u32[]{:S(2)}) async-start(f32[4,64,128]{2,0,1:T(4,128)} %copy.405), calls=%async_computation.1 | async-start | bytes 262144 | tf_op jit(solution)/shard_map/all_to_all | solution.py:102
  99.2 10.3 %all-to-all-done.1 = f32[4,64,128]{2,0,1:T(4,128)S(1)} async-done(((f32[4,64,128]{2,0,1:T(4,128)}), f32[4,64,128]{2,0,1:T(4,128)S(1)}, u32[]{:S(2)}, u32[]{:S(2)}) %all-to-all-start.1) | async-done | bytes 131104 | tf_op jit(solution)/shard_map/all_to_all | solution.py:102
  109.5 2.6 %copy.406 = f32[8192,4]{1,0:T(8,128)} copy(f32[8192,4]{0,1:T(4,128)S(1)} %bitcast.36) | data formatting | bytes 262144 | tf_op jit(solution)/shard_map/reshape | solution.py:106
  112.2 23.0 %scatter_custom_fusion.2 = f32[4,8193]{0,1:T(8,128)} fusion(s32[8192]{0:T(1024)S(1)} %bitcast.38, f32[8192,4]{1,0:T(8,128)} %copy.406, f32[]{:T(128)} %constant.244.clone.1), kind=kCustom, calls=%fused_computation.9 | custom fusion | bytes 131600 | tf_op jit(solution)/shard_map/scatter | solution.py:106
  135.2 14.8 %slice_reduce_fusion = (f32[8192]{0:T(1024)S(1)}, f32[1,8192]{0,1:T(8,128)}, f32[1,8192]{0,1:T(8,128)}, f32[1,8192]{0,1:T(8,128)}) fusion(f32[4,8193]{0,1:T(8,128)} %scatter_custom_fusion.2), kind=kLoop, calls=%fused_computation.8 | loop fusion | bytes 262144 | tf_op jit(solution)/shard_map/slice | solution.py:109
  150.0 2.8 %copy.422 = f32[1,8192]{1,0:T(1,128)S(1)} copy(f32[1,8192]{0,1:T(8,128)} %get-tuple-element.35) | data formatting | bytes 65536
  152.8 2.8 %copy.421 = f32[1,8192]{1,0:T(1,128)S(1)} copy(f32[1,8192]{0,1:T(8,128)} %get-tuple-element.36) | data formatting | bytes 65536
  155.7 2.8 %copy.423 = f32[1,8192]{1,0:T(1,128)S(1)} copy(f32[1,8192]{0,1:T(8,128)} %get-tuple-element.37) | data formatting | bytes 65536
  158.5 1.9 multiply_reduce_fusion
  164.8 4.8 %mul.732 = f32[64,256,32]{2,1,0:T(8,128)} reshape(f32[8,8,8192]{2,1,0:T(8,128)S(1)} %broadcast_multiply_fusion) | data formatting | bytes 4194304 | tf_op jit(solution)/shard_map/mul | solution.py:51
  169.6 1.6 stack.59
  171.2 20.7 %fusion = f32[256,64,8]{1,2,0:T(8,128)S(1)} fusion(f32[8,256,32]{2,0,1:T(8,128)S(1)} %stack.59, f32[64,256,32]{2,1,0:T(8,128)} %mul.732), kind=kOutput, calls=%fused_computation.6 | convolution fusion | flops 50331648 | bytes 2883584 | tf_op jit(solution)/shard_map/aes,kes->eak/dot_general | solution.py:53
  192.3 6.2 %reshape_reshape.3 = f32[4,8,8,8,8,8]{2,1,0,5,4,3:T(8,128)} reshape(f32[256,64,8]{0,2,1:T(8,128)S(1)} %copy.419) | data formatting | bytes 1048576 | tf_op jit(solution)/shard_map/reshape;reshape | solution.py:112
  202.2 1.5 fusion.15
  203.7 3.5 %slice.118 = f32[4,8,8,6,8,8]{2,1,0,5,4,3:T(8,128)S(1)} slice(f32[4,8,8,8,8,8]{2,1,0,5,4,3:T(8,128)} %reshape_reshape.3), slice={[0:4], [0:8], [0:8], [1:7], [0:8], [0:8]} | slice | bytes 786432 | tf_op jit(solution)/shard_map/slice | solution.py:67
  207.2 2.8 %collective-permute-done.1 = f32[1,8,8,1,8,8]{2,1,0,5,4,3:T(8,128)S(1)} collective-permute-done((f32[1,8,8,1,8,8]{2,1,0,5,4,3:T(8,128)S(1)}, f32[1,8,8,1,8,8]{2,1,0,5,4,3:T(8,128)S(1)}, u32[]{:S(2)}, u32[]{:S(2)}) %collective-permute-start.1) | collective-permute-done | bytes 16416 | tf_op jit(solution)/shard_map/ppermute | solution.py:31
  210.0 1.9 slice_add_fusion.1
  212.2 4.3 %collective-permute-start.2 = (f32[4,1,8,8,1,8]{2,1,0,5,4,3:T(1,128)S(1)}, f32[4,1,8,8,1,8]{2,1,0,5,4,3:T(1,128)S(1)}, u32[]{:S(2)}, u32[]{:S(2)}) collective-permute-start(f32[4,1,8,8,1,8]{2,1,0,5,4,3:T(1,128)S(1)} %get-tuple-element.26), channel_id=1, source_target_pairs={{0,1},{1,2},{2,3},{3,4},{4,5},{5,6},{6,7},{7,8},{8,9},{9,10},{10,1... | collective-permute-start | bytes 24584 | tf_op jit(solution)/shard_map/ppermute | solution.py:28
  216.6 1.9 collective-permute-start.3
  218.5 1.9 pad_maximum_fusion
  224.0 1.6 pad_maximum_fusion.1
  226.4 3.7 %pad_maximum_fusion.2 = f32[4,8,8,8,8,8]{2,1,0,5,4,3:T(8,128)} fusion(f32[4,8,8,8,8,1]{2,1,0,5,4,3:T(8,128)S(1)} %get-tuple-element.23, f32[4,8,8,8,8,6]{2,1,0,5,4,3:T(8,128)S(1)} %slice.123, f32[4,8,8,8,8,1]{2,1,0,5,4,3:T(8,128)S(1)} %get-tuple-element.22), kind=kLoop, calls=%fused_computation.5 | loop fusion | flops 262144 | bytes 1048576 | tf_op jit(solution)/shard_map/concatenate | solution.py:68
  230.2 5.9 %copy.420 = f32[4,8,8,512]{3,2,1,0:T(8,128)} copy(f32[4,8,8,512]{2,1,0,3:T(8,128)} %bitcast.26) | data formatting | bytes 1048576
  (33 shorter events, 15.4 us)
Async XLA Ops:
  38.9 52.3 %all-to-all-start = ((s32[1,64,128]{2,0,1:T(1,128)}), s32[1,64,128]{2,0,1:T(1,128)S(1)}, u32[]{:S(2)}, u32[]{:S(2)}) async-start(s32[1,64,128]{2,0,1:T(1,128)} %bitcast), calls=%async_computation | async-start | bytes 65536 | tf_op jit(solution)/shard_map/all_to_all | solution.py:103
  91.2 18.3 %all-to-all-start.1 = ((f32[4,64,128]{2,0,1:T(4,128)}), f32[4,64,128]{2,0,1:T(4,128)S(1)}, u32[]{:S(2)}, u32[]{:S(2)}) async-start(f32[4,64,128]{2,0,1:T(4,128)} %copy.405), calls=%async_computation.1 | async-start | bytes 262144 | tf_op jit(solution)/shard_map/all_to_all | solution.py:102
  164.8 4.8 %copy-start = (f32[1,256,32]{2,1,0:T(8,128)S(1)}, f32[1,256,32]{2,1,0:T(8,128)}, u32[]{:S(2)}) copy-start(f32[1,256,32]{2,1,0:T(8,128)} %stack.24) | copy-start | bytes 98308
  199.6 7.6 %collective-permute-start = (f32[1,8,8,1,8,8]{2,1,0,5,4,3:T(8,128)S(1)}, f32[1,8,8,1,8,8]{2,1,0,5,4,3:T(8,128)S(1)}, u32[]{:S(2)}, u32[]{:S(2)}) collective-permute-start(f32[1,8,8,1,8,8]{2,1,0,5,4,3:T(8,128)S(1)} %get-tuple-element.30), channel_id=1, source_target_pairs={{0,64},{64,128},{128,192},{1,65},{65,129},{129,193},{2,66},{66,130... | collective-permute-start | bytes 49160 | tf_op jit(solution)/shard_map/ppermute | solution.py:28
  200.9 9.1 %collective-permute-start.1 = (f32[1,8,8,1,8,8]{2,1,0,5,4,3:T(8,128)S(1)}, f32[1,8,8,1,8,8]{2,1,0,5,4,3:T(8,128)S(1)}, u32[]{:S(2)}, u32[]{:S(2)}) collective-permute-start(f32[1,8,8,1,8,8]{2,1,0,5,4,3:T(8,128)S(1)} %get-tuple-element.31), channel_id=1, source_target_pairs={{64,0},{128,64},{192,128},{65,1},{129,65},{193,129},{66,2},{130,66... | collective-permute-start | bytes 49160 | tf_op jit(solution)/shard_map/ppermute | solution.py:31
  212.2 9.4 %collective-permute-start.2 = (f32[4,1,8,8,1,8]{2,1,0,5,4,3:T(1,128)S(1)}, f32[4,1,8,8,1,8]{2,1,0,5,4,3:T(1,128)S(1)}, u32[]{:S(2)}, u32[]{:S(2)}) collective-permute-start(f32[4,1,8,8,1,8]{2,1,0,5,4,3:T(1,128)S(1)} %get-tuple-element.26), channel_id=1, source_target_pairs={{0,1},{1,2},{2,3},{3,4},{4,5},{5,6},{6,7},{7,8},{8,9},{9,10},{10,1... | collective-permute-start | bytes 24584 | tf_op jit(solution)/shard_map/ppermute | solution.py:28
  216.6 6.3 %collective-permute-start.3 = (f32[4,1,8,8,1,8]{2,1,0,5,4,3:T(1,128)S(1)}, f32[4,1,8,8,1,8]{2,1,0,5,4,3:T(1,128)S(1)}, u32[]{:S(2)}, u32[]{:S(2)}) collective-permute-start(f32[4,1,8,8,1,8]{2,1,0,5,4,3:T(1,128)S(1)} %get-tuple-element.27), channel_id=1, source_target_pairs={{1,0},{2,1},{3,2},{4,3},{5,4},{6,5},{7,6},{8,7},{9,8},{10,9},{11,1... | collective-permute-start | bytes 24584 | tf_op jit(solution)/shard_map/ppermute | solution.py:31
where the time goes:
time: 237 us; the launch traced here: 236 us
  local copies, waits for them, and re-layouts  111 us (47%)
  blocking collectives  40.2 us (17%)
  starting transfers between devices  30.6 us (13%)
  matrix products  20.7 us (9%)
  other arithmetic  17.6 us (7%)
  waiting for transfers between devices  14.3 us (6%)
    psum x4, blocking collectives, by_axis(): return functools.reduce(lax.psum, axes, array)  40.2 us
    scatter x1, local copies, waits for them, and re-layouts, on_device(): packed.at[:, got_cells.reshape(-1)].set(got_values.reshape(channels, -1))  23 us
    dot_general x1, matrix products, contract(): jnp.einsum('aes,kes->eak', outer, third, precision=lax.Precision.HIGHEST)  20.7 us
    scatter x1, local copies, waits for them, and re-layouts, on_device(): jnp.full((peer_count * capacity,), cell_count, jnp.int32).at[target]  16.1 us
    slice x1, local copies, waits for them, and re-layouts, on_device(): first_w = basis_values(packed[0]) * packed[3]  14.8 us
    unnamed x6, local copies, waits for them, and re-layouts  14.4 us
    all_to_all x1, starting transfers between devices, on_device(): lax.all_to_all(send_cells, DEV, split_axis=1, concat_axis=1, tiled=True)  13.8 us
    scatter x1, local copies, waits for them, and re-layouts, on_device(): jnp.zeros((channels, peer_count * capacity), payload.dtype).at[:, target]  12.8 us
  transfers between devices with their start and end apart: 6, of which 3 were waited for; matrix products, arithmetic and copies ran while one was open for 11% of the time, Pallas kernels for 0%

commit v1 on v0

v1 whole, which is shorter than its diff:
```python
import functools
import math

import jax
import jax.numpy as jnp
from jax import lax
from jax.experimental import pallas as pl
from jax.experimental.pallas import tpu as pltpu
from jax.sharding import PartitionSpec as P

CAP = 128
ELEM = 256
NODES = 512
COPLANE = 16
NODE_POINTS = [-math.cos(math.pi * k / 7) for k in range(8)]
NODE_SCALE = [
    1.0 / math.prod(NODE_POINTS[a] - NODE_POINTS[m] for m in range(8) if m != a)
    for a in range(8)
]
NT = (((1,), (1,)), ((), ()))


def peer_order(n_dev):
    def hops(offset):
        y, z = offset // COPLANE, (offset % COPLANE) // 2
        return min(y, max(n_dev // COPLANE, 1) - y) + min(z, COPLANE // 2 - z)

    return [0] + sorted(range(1, n_dev), key=lambda o: (hops(o), o))


def lanes_of(shape):
    return lax.broadcasted_iota(jnp.int32, shape, len(shape) - 1)


def rows_of(shape):
    return lax.broadcasted_iota(jnp.int32, shape, len(shape) - 2)


def split(value):
    high = value.astype(jnp.bfloat16).astype(jnp.float32)
    return high, value - high


def basis(t):
    shape = (8, t.shape[1])
    t = jnp.broadcast_to(t, shape)
    row = rows_of(shape)
    out = None
    for m in range(8):
        factor = jnp.where(row == m, jnp.float32(NODE_SCALE[m]), t - jnp.float32(NODE_POINTS[m]))
        out = factor if out is None else out * factor
    return out


def kernel(
    n_grp, n_dev, coord, resid, weight, dest, slot, elem, out, cost,
    coord_v, resid_v, weight_v, dest_v, slot_v, elem_v,
    lhs, pick, send, recv, xa, xb, oha, ohb, acc, fin,
    c1s, c1r, c2s, c2r, halo_g, halo_d, halo_c, dsend,
    in_sem, send_sem, recv_sem, c1_ssem, c1_rsem, c2_ssem, c2_rsem, h_ssem, h_rsem,
):
    g, d = lax.axis_index("grp"), lax.axis_index("dev")
    co = min(COPLANE, n_dev)
    planes = n_dev // co
    order = peer_order(n_dev)
    here = lax.rem(d, co)
    block = d - here

    def at(dg, dd):
        return {"grp": lax.rem(g + dg + n_grp, n_grp), "dev": lax.rem(d + dd + n_dev, n_dev)}

    barrier = pltpu.get_barrier_semaphore()
    corners = [(-1, -1), (-1, 1), (1, -1), (1, 1)]
    peers = [(0, o) for o in order[1:]]
    peers += [(k, p * co) for k in range(1, n_grp) for p in range(planes)]
    peers += corners
    for dg, dd in peers:
        pl.semaphore_signal(barrier, inc=1, device_id=at(dg, dd))

    loads = [
        pltpu.make_async_copy(src, dst, in_sem.at[i])
        for i, (src, dst) in enumerate(
            [(dest, dest_v), (slot, slot_v), (elem, elem_v), (coord, coord_v), (resid, resid_v), (weight, weight_v)]
        )
    ]
    for load in loads:
        load.start()
    for load in loads:
        load.wait()

    def fill(j, carry):
        def pair(ref):
            return jnp.concatenate([ref[pl.ds(2 * j, 1), :], ref[pl.ds(2 * j + 1, 1), :]], axis=1)

        cols = pl.ds(pl.multiple_of(j * 256, 256), 256)
        here_mask = rows_of((n_dev, 256)) == pair(dest_v)
        vals = [coord_v[c : c + 1, cols] for c in range(3)]
        vals.append(pair(weight_v) * pair(resid_v))
        for c, value in enumerate(vals):
            for h, part in enumerate(split(value)):
                row = (2 * c + h) * n_dev
                lhs[row : row + n_dev, cols] = jnp.where(here_mask, part, 0.0).astype(jnp.bfloat16)
        ids = pair(elem_v).astype(jnp.float32)
        lhs[8 * n_dev : 9 * n_dev, cols] = jnp.where(here_mask, ids, 0.0).astype(jnp.bfloat16)
        slot_mask = rows_of((CAP, 256)) == pair(slot_v)
        pick[:, cols] = jnp.where(slot_mask, 1.0, 0.0).astype(jnp.bfloat16)
        return carry

    lax.fori_loop(0, resid_v.shape[0] // 2, fill, 0)
    packed = lax.dot_general(lhs[...], pick[...], NT, preferred_element_type=jnp.float32)
    part = [packed[k * n_dev : (k + 1) * n_dev] for k in range(9)]
    for c in range(4):
        send[:, c, :] = part[2 * c] + part[2 * c + 1]
    send[:, 4, :] = part[8]
    r = resid_v[...]
    c1s[...] = jnp.sum(weight_v[...] * r * r, axis=0, keepdims=True)

    recv[0] = send[d]
    c1r[here] = c1s[...]

    pl.semaphore_wait(barrier, len(peers))

    def message(k):
        return pltpu.make_async_remote_copy(
            src_ref=send.at[lax.rem(d + order[k], n_dev)],
            dst_ref=recv.at[k],
            send_sem=send_sem.at[k],
            recv_sem=recv_sem.at[k],
            device_id=at(0, order[k]),
        )

    messages = [message(k) for k in range(1, n_dev)]
    for m in reversed(messages):
        m.start()

    def partial_one(k):
        return pltpu.make_async_remote_copy(
            src_ref=c1s, dst_ref=c1r.at[here], send_sem=c1_ssem.at[k], recv_sem=c1_rsem.at[k],
            device_id={"grp": g, "dev": block + lax.rem(here + k, co)},
        )

    ones = [partial_one(k) for k in range(1, co)]
    for m in ones:
        m.start()

    acc[...] = jnp.zeros_like(acc)
    xb[...] = jnp.zeros_like(xb)
    ohb[...] = jnp.zeros_like(ohb)

    def build(p, x, oh):
        first, second = recv[2 * p], recv[2 * p + 1]

        def row(c):
            return jnp.concatenate([first[c : c + 1], second[c : c + 1]], axis=1)

        fa = basis(row(0)) * row(3)
        fb = basis(row(1))
        fc = basis(row(2))
        for a in range(8):
            ab = fa[a : a + 1] * fb
            for b in range(0, 8, 2):
                full = jnp.concatenate([ab[b : b + 1] * fc, ab[b + 1 : b + 2] * fc], axis=0)
                high = full.astype(jnp.bfloat16)
                low = (full - high.astype(jnp.float32)).astype(jnp.bfloat16)
                at_row = (8 * a + b) * 8
                x[at_row : at_row + 16, 0:256] = high
                x[at_row : at_row + 16, 256:512] = low
        ids = row(4).astype(jnp.int32)
        oh[...] = jnp.where(rows_of((ELEM, 256)) == ids, 1.0, 0.0).astype(jnp.bfloat16)

    def product(x, oh):
        return lax.dot_general(
            x[:, 0:256], oh[...], NT, preferred_element_type=jnp.float32
        ) + lax.dot_general(x[:, 256:512], oh[...], NT, preferred_element_type=jnp.float32)

    def arrived(k):
        pltpu.make_async_remote_copy(
            src_ref=send.at[0], dst_ref=recv.at[k], send_sem=send_sem.at[k], recv_sem=recv_sem.at[k],
            device_id=at(0, 1),
        ).wait_recv()

    def two_pairs(t):
        acc[...] += product(xb, ohb)
        build(2 * t, xa, oha)
        acc[...] += product(xa, oha)
        build(2 * t + 1, xb, ohb)

    for k in range(1, 4):
        arrived(k)
    two_pairs(0)

    def body(t, carry):
        for k in range(4):
            arrived(4 * t + k)
        two_pairs(t)
        return carry

    if n_dev > 4:
        lax.fori_loop(1, n_dev // 4, body, 0)
    acc[...] += product(xb, ohb)

    lane = lanes_of((8, ELEM))

    def rg(ref, a, b):
        return ref[(8 * a + b) * 8 : (8 * a + b) * 8 + 8, :]

    def put(ref, a, b, value):
        ref[(8 * a + b) * 8 : (8 * a + b) * 8 + 8, :] = value

    def move(x, k):
        return pltpu.roll(x, k % x.shape[1], 1)

    for b in range(8):
        low, high = rg(acc, 0, b), rg(acc, 7, b)
        put(acc, 0, b, low + jnp.where(lane >= 64, move(high, 64), 0.0))
        put(acc, 7, b, high + jnp.where(lane < 192, move(low, -64), 0.0))
    half = lanes_of((8, 128))
    for a in range(8):
        for side, b in ((0, 0), (1, 7)):
            x = rg(acc, a, b)
            near = ((half >> 3) & 7) == b
            left = jnp.where(near, x[:, :128], 0.0)
            right = jnp.where(near, x[:, 128:], 0.0)
            dsend[side, 8 * a : 8 * a + 8, :] = left + move(right, 8 if b == 0 else -8)

    for k in range(1, co):
        pltpu.make_async_remote_copy(
            src_ref=c1s, dst_ref=c1r.at[here], send_sem=c1_ssem.at[k], recv_sem=c1_rsem.at[k],
            device_id=at(0, 1),
        ).wait_recv()
    total = c1r[0]
    for k in range(1, co):
        total += c1r[k]
    c2s[...] = total
    mine = g * planes + block // co
    c2r[mine] = total

    def halo(i, src, dst, dg, dd):
        return pltpu.make_async_remote_copy(
            src_ref=src, dst_ref=dst, send_sem=h_ssem.at[i], recv_sem=h_rsem.at[i],
            device_id=at(dg, dd),
        )

    halos = [
        halo(0, acc.at[0:64, 0:128], halo_g.at[0], -1, 0),
        halo(1, acc.at[448:512, 128:256], halo_g.at[1], 1, 0),
        halo(2, dsend.at[0], halo_d.at[0], 0, -1),
        halo(3, dsend.at[1], halo_d.at[1], 0, 1),
        halo(4, acc.at[0:8, 0:128], halo_c.at[0], -1, -1),
        halo(5, acc.at[56:64, 0:128], halo_c.at[1], -1, 1),
        halo(6, acc.at[448:456, 128:256], halo_c.at[2], 1, -1),
        halo(7, acc.at[504:512, 128:256], halo_c.at[3], 1, 1),
    ]
    for m in halos:
        m.start()
    rest = [(k, p) for k in range(n_grp) for p in range(planes) if k or p]
    twos = [
        pltpu.make_async_remote_copy(
            src_ref=c2s, dst_ref=c2r.at[mine], send_sem=c2_ssem.at[i], recv_sem=c2_rsem.at[i],
            device_id=at(k, p * co),
        )
        for i, (k, p) in enumerate(rest)
    ]
    for m in twos:
        m.start()
    for m in halos:
        m.wait_recv()

    up_g, down_g = g > 0, g < n_grp - 1
    up_d, down_d = d > 0, d < n_dev - 1
    ey = (lane >> 3) & 7
    ez = lane & 7

    def wide(x):
        return jnp.concatenate([x, x], axis=1)

    for b in range(8):
        from_low = move(halo_g[1, 8 * b : 8 * b + 8, :], 64)
        from_high = move(halo_g[0, 8 * b : 8 * b + 8, :], 64)
        put(fin, 0, b, rg(acc, 0, b) + jnp.where((lane < 64) & up_g, wide(from_low), 0.0))
        put(fin, 7, b, rg(acc, 7, b) + jnp.where((lane >= 192) & down_g, wide(from_high), 0.0))
    for a in range(1, 7):
        fin[64 * a : 64 * a + 64, :] = acc[64 * a : 64 * a + 64, :]
    for a in range(8):
        low, high = rg(fin, a, 0), rg(fin, a, 7)
        theirs = halo_d[1, 8 * a : 8 * a + 8, :]
        to_low = jnp.concatenate([move(theirs, -56), move(theirs, -48)], axis=1)
        theirs = halo_d[0, 8 * a : 8 * a + 8, :]
        to_high = jnp.concatenate([move(theirs, 56), move(theirs, 48)], axis=1)
        if a == 0:
            to_low += jnp.where((lane < 8) & up_g, wide(move(halo_c[3], -120)), 0.0)
            to_high += jnp.where((lane >= 56) & (lane < 64) & up_g, wide(move(halo_c[2], -8)), 0.0)
        if a == 7:
            to_low += jnp.where((lane >= 192) & (lane < 200) & down_g, wide(move(halo_c[1], 8)), 0.0)
            to_high += jnp.where((lane >= 248) & down_g, wide(move(halo_c[0], 120)), 0.0)
        new_low = jnp.where(ey > 0, move(high, 8), jnp.where(up_d, to_low, 0.0))
        new_high = jnp.where(ey < 7, move(low, -8), jnp.where(down_d, to_high, 0.0))
        put(fin, a, 0, low + new_low)
        put(fin, a, 7, high + new_high)
    row = rows_of((8, ELEM))
    for a in range(8):
        for b in range(8):
            x = rg(fin, a, b)
            z = jnp.where(row == 7, move(x, 1), move(x, -1))
            to_low = jnp.where((row == 0) & (ez > 0), pltpu.roll(z, 1, 0), 0.0)
            to_high = jnp.where((row == 7) & (ez < 7), pltpu.roll(z, 7, 0), 0.0)
            put(fin, a, b, x + to_low + to_high)
    out[...] = fin[...].T

    for m in twos:
        m.wait_recv()
    total = c2r[0]
    for k in range(1, n_grp * planes):
        total += c2r[k]
    cost[0, 0] = 0.5 * jnp.sum(total)
    for m in messages + ones + halos + twos:
        m.wait_send()


def on_device(coord, resid, weight, dest, slot, elem, n_grp, n_dev):
    rows = resid.shape[0] // 128
    flat = [x.reshape(rows, 128) for x in (resid, weight, dest, slot, elem)]
    co = min(COPLANE, n_dev)
    blocks = n_grp * (n_dev // co)
    f32, bf16, i32 = jnp.float32, jnp.bfloat16, jnp.int32
    dma = pltpu.SemaphoreType.DMA
    out, cost = pl.pallas_call(
        functools.partial(kernel, n_grp, n_dev),
        out_shape=(
            jax.ShapeDtypeStruct((ELEM, NODES), f32),
            jax.ShapeDtypeStruct((1, 1), f32),
        ),
        in_specs=[pl.BlockSpec(memory_space=pl.ANY)] * 6,
        out_specs=(
            pl.BlockSpec(memory_space=pltpu.VMEM),
            pl.BlockSpec(memory_space=pltpu.SMEM),
        ),
        scratch_shapes=[
            pltpu.VMEM(coord.shape, f32),
            pltpu.VMEM((rows, 128), f32),
            pltpu.VMEM((rows, 128), f32),
            pltpu.VMEM((rows, 128), i32),
            pltpu.VMEM((rows, 128), i32),
            pltpu.VMEM((rows, 128), i32),
            pltpu.VMEM((9 * n_dev, rows * 128), bf16),
            pltpu.VMEM((CAP, rows * 128), bf16),
            pltpu.VMEM((n_dev, 5, CAP), f32),
            pltpu.VMEM((n_dev, 5, CAP), f32),
            pltpu.VMEM((NODES, 512), bf16),
            pltpu.VMEM((NODES, 512), bf16),
            pltpu.VMEM((ELEM, 256), bf16),
            pltpu.VMEM((ELEM, 256), bf16),
            pltpu.VMEM((NODES, ELEM), f32),
            pltpu.VMEM((NODES, ELEM), f32),
            pltpu.VMEM((1, 128), f32),
            pltpu.VMEM((co, 1, 128), f32),
            pltpu.VMEM((1, 128), f32),
            pltpu.VMEM((blocks, 1, 128), f32),
            pltpu.VMEM((2, 64, 128), f32),
            pltpu.VMEM((2, 64, 128), f32),
            pltpu.VMEM((4, 8, 128), f32),
            pltpu.VMEM((2, 64, 128), f32),
            dma((6,)),
            dma((n_dev,)),
            dma((n_dev,)),
            dma((co,)),
            dma((co,)),
            dma((blocks,)),
            dma((blocks,)),
            dma((8,)),
            dma((8,)),
        ],
        compiler_params=pltpu.CompilerParams(collective_id=0, has_side_effects=True),
    )(coord, *flat)
    return out.reshape(4, 8, 8, NODES), cost.reshape(())


def solution(mesh):
    n_grp, n_dev = mesh.shape["grp"], mesh.shape["dev"]
    rows = P(("grp", "dev"))

    def step(obs_coord, obs_resid, obs_weight, obs_dest, obs_send_slot, obs_elem, obs_slot):
        del obs_slot
        return on_device(
            obs_coord, obs_resid, obs_weight, obs_dest, obs_send_slot, obs_elem, n_grp, n_dev
        )

    return jax.shard_map(
        step,
        mesh=mesh,
        in_specs=(P(None, ("grp", "dev")), rows, rows, rows, rows, rows, rows),
        out_specs=(P("grp", "dev", None, None), P()),
        check_vma=False,
    )
```

time: 237 us -> 40.6 us (0.17)
  local copies, waits for them, and re-layouts: 111 us -> 1.87 us
  blocking collectives: 40.2 us -> 0 us
  Pallas kernels: 0 us -> 36.2 us
  starting transfers between devices: 30.6 us -> 0 us
  matrix products: 20.7 us -> 0 us
  other arithmetic: 17.6 us -> 0 us
  waiting for transfers between devices: 14.3 us -> 0 us
    scatter x3 -> x0, local copies, waits for them, and re-layouts: 51.9 us -> none  [the longest x1 23 us: on_device(): packed.at[:, got_cells.reshape(-1)].set(got_values.reshape(channels, -1))]
    psum x4 -> x0, blocking collectives: 40.2 us -> none  [by_axis(): return functools.reduce(lax.psum, axes, array)]
    pallas_call x0 -> x1, Pallas kernels: none -> 36.2 us  [on_device(): pl.pallas_call(functools.partial(kernel, n_grp, n_dev), out_shape=(jax.Sh...]
    slice x6 -> x0, local copies, waits for them, and re-layouts: 22.9 us -> none  [the longest x1 14.8 us: on_device(): first_w = basis_values(packed[0]) * packed[3]]
    all_to_all x2 -> x0, starting transfers between devices: 21.8 us -> none  [the longest x1 13.8 us: on_device(): lax.all_to_all(send_cells, DEV, split_axis=1, concat_axis=1, tiled=True)]
    dot_general x1 -> x0, matrix products: 20.7 us -> none  [contract(): jnp.einsum('aes,kes->eak', outer, third, precision=lax.Precision.HIGHEST)]
    unnamed x6 -> x1, local copies, waits for them, and re-layouts: 14.4 us -> 1.87 us
    all_to_all x2 -> x0, waiting for transfers between devices: 10.3 us -> none  [the longest x1 10.3 us: on_device(): lax.all_to_all(send_values, DEV, split_axis=1, concat_axis=1, tiled=True)]
  transfers between devices with their start and end apart: 6 -> 0, of which waited for: 3 -> 0; matrix products, arithmetic and copies ran while one was open for 11% -> 0% of each run, Pallas kernels for 0% -> 0%
where the time goes in v1:
time: 40.6 us; the launch traced here: 40.4 us
  Pallas kernels  36.2 us (89%)
  between operations  2.34 us (6%)
  local copies, waits for them, and re-layouts  1.87 us (5%)
    pallas_call x1, Pallas kernels, on_device(): pl.pallas_call(functools.partial(kernel, n_grp, n_dev), out_shape=(jax.Sh...  36.2 us
    unnamed x1, local copies, waits for them, and re-layouts  1.87 us

profile of v1, /device:TPU:1, one launch (start us, length us, event | category | flops | bytes accessed | tf_op | source)
XLA Modules:
  0.0 40.4 jit_solution(3602351565054967773)
XLA Ops:
  0.6 36.2 %shard_map.77 = (f32[256,512]{1,0:T(8,128)}, f32[1,1]{1,0:T(1,128)}) custom-call(f32[3,4096]{1,0:T(4,128)} %coord.1, f32[32,128]{1,0:T(8,128)} %bitcast.8, f32[32,128]{1,0:T(8,128)} %bitcast.9, s32[32,128]{1,0:T(8,128)} %bitcast.10, s32[32,128]{1,0:T(8,128)} %bitcast.11, s32[32,128]{1,0:T(8,128)} %bitcast.12), custom_call_target="tpu_custom_call" | custom-call | tf_op jit(solution)/shard_map/pallas_call | solution.py:327
  36.8 1.9 %copy.10 = f32[4,8,8,512]{3,2,1,0:T(8,128)} copy(f32[4,8,8,512]{3,2,1,0:T(8,128)} %bitcast.7) | data formatting | bytes 1048576

commit v2 on v1

v2 whole, which is shorter than its diff:
```python
import functools
import math

import jax
import jax.numpy as jnp
from jax import lax
from jax.experimental import pallas as pl
from jax.experimental.pallas import tpu as pltpu
from jax.sharding import PartitionSpec as P

CAP = 128
ELEM = 256
NODES = 512
COPLANE = 16
PEERS = 64
NODE_POINTS = [-math.cos(math.pi * k / 7) for k in range(8)]
NODE_SCALE = [
    1.0 / math.prod(NODE_POINTS[a] - NODE_POINTS[m] for m in range(8) if m != a)
    for a in range(8)
]
NT = (((1,), (1,)), ((), ()))
F32, BF16, I32 = jnp.float32, jnp.bfloat16, jnp.int32
EDGE = (0, 7)
OUTER = [(a, b) for a in range(8) for b in range(8) if a in EDGE or b in EDGE]
INNER = [(a, b) for a in range(8) for b in range(8) if not (a in EDGE or b in EDGE)]
OUTER.sort(key=lambda ab: (EDGE.index(ab[0]) if ab[0] in EDGE else 2, ab))
GROUPS = OUTER + INNER
PLACE = {ab: 8 * i for i, ab in enumerate(GROUPS)}
SPLIT = 8 * len(OUTER)


def peer_order(n_dev):
    def hops(offset):
        y, z = offset // COPLANE, (offset % COPLANE) // 2
        return min(y, max(n_dev // COPLANE, 1) - y) + min(z, COPLANE // 2 - z)

    return [0] + sorted(range(1, n_dev), key=lambda o: (hops(o), o))


def lanes_of(shape):
    return lax.broadcasted_iota(I32, shape, len(shape) - 1)


def rows_of(shape):
    return lax.broadcasted_iota(I32, shape, len(shape) - 2)


def high_of(value):
    return value.astype(BF16).astype(F32)


def one_hot(ids, count):
    shape = (count, ids.shape[1])
    ids = jnp.broadcast_to(ids, (16, ids.shape[1])).astype(BF16)
    ids = jnp.concatenate([ids] * (count // 16), axis=0)
    row = rows_of(shape).astype(F32).astype(BF16)
    return jnp.where(row == ids, jnp.ones(shape, BF16), jnp.zeros(shape, BF16))


def basis(t):
    shape = (8, t.shape[1])
    t = jnp.broadcast_to(t, shape)
    row = rows_of(shape)
    out = None
    for m in range(8):
        factor = jnp.where(row == m, F32(NODE_SCALE[m]), t - F32(NODE_POINTS[m]))
        out = factor if out is None else out * factor
    return out


def move(x, k):
    return pltpu.roll(x, k % x.shape[1], 1)


def exchange_kernel(
    n_grp, n_dev, coord, resid, weight, dest, slot, elem, mid, cost,
    coord_v, resid_v, weight_v, dest_v, slot_v, elem_v,
    lhs, pick, send, recv, xo, xi, oh, acc, outer,
    c1s, c1r, c2s, c2r, halo_g, halo_d, halo_c, dsend,
    in_sem, send_sem, recv_sem, c1_ssem, c1_rsem, c2_ssem, c2_rsem, h_ssem, h_rsem,
):
    g, d = lax.axis_index("grp"), lax.axis_index("dev")
    co = min(COPLANE, n_dev)
    planes = n_dev // co
    order = peer_order(n_dev)
    here = lax.rem(d, co)
    block = d - here

    def at(dg, dd):
        return {"grp": lax.rem(g + dg + n_grp, n_grp), "dev": lax.rem(d + dd + n_dev, n_dev)}

    loads = [
        pltpu.make_async_copy(src, dst, in_sem.at[i])
        for i, (src, dst) in enumerate(
            [(dest, dest_v), (slot, slot_v), (elem, elem_v), (coord, coord_v), (resid, resid_v), (weight, weight_v)]
        )
    ]
    for load in loads:
        load.start()

    barrier = pltpu.get_barrier_semaphore()
    corners = [(-1, -1), (-1, 1), (1, -1), (1, 1)]
    peers = [(k, p * co) for k in range(1, n_grp) for p in range(planes)]
    peers += corners
    peers += [(0, o) for o in order[1:]]
    for dg, dd in reversed(peers):
        pl.semaphore_signal(barrier, inc=1, device_id=at(dg, dd))
    for load in loads:
        load.wait()

    for j in range(resid_v.shape[0] // 2):
        def pair(ref):
            return jnp.concatenate([ref[2 * j : 2 * j + 1, :], ref[2 * j + 1 : 2 * j + 2, :]], axis=1)

        cols = slice(256 * j, 256 * j + 256)
        to = pair(dest_v)
        upper = to >> 5
        mask = one_hot((to - 32 * upper).astype(F32), 32)
        pick[:, cols] = one_hot((upper * CAP + pair(slot_v)).astype(F32), 256)
        parts = []
        for value in [coord_v[c : c + 1, cols] for c in range(3)] + [pair(weight_v) * pair(resid_v)]:
            high = high_of(value)
            parts += [high, value - high]
        parts.append(pair(elem_v).astype(F32))
        for i, part in enumerate(parts):
            wide = jnp.broadcast_to(part, (16, 256)).astype(BF16)
            lhs[32 * i : 32 * i + 32, cols] = mask * jnp.concatenate([wide, wide], axis=0)
    packed = lax.dot_general(lhs[...], pick[...], NT, preferred_element_type=F32)
    part = [packed[32 * k : 32 * k + 32] for k in range(9)]
    values = [part[2 * c] + part[2 * c + 1] for c in range(4)] + [part[8]]
    for c, value in enumerate(values):
        send[0:32, c, :] = value[:, :CAP]
        send[32:64, c, :] = value[:, CAP:]
    r = resid_v[...]
    c1s[...] = jnp.sum(weight_v[...] * r * r, axis=0, keepdims=True)

    recv[0] = send[d]
    c1r[here] = c1s[...]

    pl.semaphore_wait(barrier, len(peers))

    bounds = [0, 24, 44, 56, 64] if n_dev == 64 else [0, 2, 4]
    chunks = list(zip(bounds[:-1], bounds[1:]))
    chunk_of = [i for i, (first, last) in enumerate(chunks) for _ in range(first, last)]

    def message(k):
        to = lax.rem(d + order[k], n_dev)
        return pltpu.make_async_remote_copy(
            src_ref=send.at[to],
            dst_ref=recv.at[k],
            send_sem=send_sem,
            recv_sem=recv_sem.at[chunk_of[k]],
            device_id={"grp": g, "dev": to},
        )

    def await_bytes(ref, sem):
        pltpu.make_async_copy(ref, ref, sem).wait()

    for k in range(1, n_dev):
        message(k).start()

    def partial_one(k):
        return pltpu.make_async_remote_copy(
            src_ref=c1s, dst_ref=c1r.at[here], send_sem=c1_ssem, recv_sem=c1_rsem,
            device_id={"grp": g, "dev": block + lax.rem(here + k, co)},
        )

    for k in range(1, co):
        partial_one(k).start()

    mine = g * planes + block // co
    rest = [(k, p) for k in range(n_grp) for p in range(planes) if k or p]
    twos = [
        pltpu.make_async_remote_copy(
            src_ref=c2s, dst_ref=c2r.at[mine], send_sem=c2_ssem, recv_sem=c2_rsem,
            device_id=at(k, p * co),
        )
        for k, p in rest
    ]

    def build(p):
        first, second = recv[2 * p], recv[2 * p + 1]

        def row(c):
            return jnp.concatenate([first[c : c + 1], second[c : c + 1]], axis=1)

        cols = slice(256 * p, 256 * p + 256)
        fa = basis(row(0)) * row(3)
        fb = basis(row(1))
        fc = basis(row(2))
        for i in range(0, 64, 2):
            full = jnp.concatenate(
                [fa[a : a + 1] * fb[b : b + 1] * fc for a, b in GROUPS[i : i + 2]], axis=0
            )
            high = full.astype(BF16)
            low = (full - high.astype(F32)).astype(BF16)
            ref, row_of, count = (xo, 8 * i, SPLIT) if 8 * i < SPLIT else (xi, 8 * i - SPLIT, NODES - SPLIT)
            ref[row_of : row_of + 16, cols] = high
            ref[count + row_of : count + row_of + 16, cols] = low
        oh[:, cols] = one_hot(row(4), ELEM)

    def product(ref, cols):
        return lax.dot_general(ref[:, cols], oh[:, cols], NT, preferred_element_type=F32)

    def arrived(i):
        first, last = max(chunks[i][0], 1), chunks[i][1]
        await_bytes(recv.at[first:last], recv_sem.at[i])

    def cols_of(first, last):
        return slice(128 * first, 128 * last)

    arrived(0)
    for p in range(chunks[0][0] // 2, chunks[0][1] // 2):
        build(p)
    for i, chunk in enumerate(chunks):
        if i + 1 < len(chunks):
            arrived(i + 1)
        now = product(xo, cols_of(*chunk))
        if i > 0:
            now = acc[...] + now
        if i + 1 < len(chunks):
            acc[...] = now
            for p in range(chunks[i + 1][0] // 2, chunks[i + 1][1] // 2):
                build(p)
        else:
            outer[...] = now[:SPLIT] + now[SPLIT:]
        if i == 1:
            await_bytes(c1r.at[1:co], c1_rsem)
            total = c1r[0]
            for k in range(1, co):
                total += c1r[k]
            c2s[...] = total
            c2r[mine] = total
            for m in twos:
                m.start()

    lane = lanes_of((8, ELEM))

    def rg(ref, a, b):
        return ref[PLACE[a, b] : PLACE[a, b] + 8, :]

    def put(ref, a, b, value):
        ref[PLACE[a, b] : PLACE[a, b] + 8, :] = value

    for b in range(8):
        low, high = rg(outer, 0, b), rg(outer, 7, b)
        put(outer, 0, b, low + jnp.where(lane >= 64, move(high, 64), 0.0))
        put(outer, 7, b, high + jnp.where(lane < 192, move(low, -64), 0.0))
    half = lanes_of((8, 128))
    for a in range(8):
        for side, b in ((0, 0), (1, 7)):
            plane = rg(outer, a, b)
            near = ((half >> 3) & 7) == b
            left = jnp.where(near, plane[:, :128], 0.0)
            right = jnp.where(near, plane[:, 128:], 0.0)
            dsend[side, 8 * a : 8 * a + 8, :] = left + move(right, 8 if b == 0 else -8)

    def halo(kind, src, dst, dg, dd):
        return pltpu.make_async_remote_copy(
            src_ref=src, dst_ref=dst, send_sem=h_ssem.at[kind], recv_sem=h_rsem.at[kind],
            device_id=at(dg, dd),
        )

    def tile(a, b, count, right):
        first = PLACE[a, b]
        return outer.at[first : first + 8 * count, (128 if right else 0) : (256 if right else 128)]

    halos = [
        halo(0, tile(0, 0, 8, False), halo_g.at[0], -1, 0),
        halo(0, tile(7, 0, 8, True), halo_g.at[1], 1, 0),
        halo(1, dsend.at[0], halo_d.at[0], 0, -1),
        halo(1, dsend.at[1], halo_d.at[1], 0, 1),
        halo(2, tile(0, 0, 1, False), halo_c.at[0], -1, -1),
        halo(2, tile(0, 7, 1, False), halo_c.at[1], -1, 1),
        halo(2, tile(7, 0, 1, True), halo_c.at[2], 1, -1),
        halo(2, tile(7, 7, 1, True), halo_c.at[3], 1, 1),
    ]
    for m in halos:
        m.start()
    left = product(xi, slice(0, n_dev * CAP))
    mid[SPLIT:, :] = left[: NODES - SPLIT] + left[NODES - SPLIT :]

    for kind, ref in enumerate((halo_g, halo_d, halo_c)):
        await_bytes(ref, h_rsem.at[kind])

    up_g, down_g = g > 0, g < n_grp - 1
    up_d, down_d = d > 0, d < n_dev - 1
    ey = (lane >> 3) & 7

    def wide(value):
        return jnp.concatenate([value, value], axis=1)

    planes_now = {ab: rg(outer, *ab) for ab in OUTER}
    for b in range(8):
        from_low = move(halo_g[1, 8 * b : 8 * b + 8, :], 64)
        from_high = move(halo_g[0, 8 * b : 8 * b + 8, :], 64)
        planes_now[0, b] += jnp.where((lane < 64) & up_g, wide(from_low), 0.0)
        planes_now[7, b] += jnp.where((lane >= 192) & down_g, wide(from_high), 0.0)
    for a in range(8):
        low, high = planes_now[a, 0], planes_now[a, 7]
        theirs = halo_d[1, 8 * a : 8 * a + 8, :]
        to_low = jnp.concatenate([move(theirs, -56), move(theirs, -48)], axis=1)
        theirs = halo_d[0, 8 * a : 8 * a + 8, :]
        to_high = jnp.concatenate([move(theirs, 56), move(theirs, 48)], axis=1)
        if a == 0:
            to_low += jnp.where((lane < 8) & up_g, wide(move(halo_c[3], -120)), 0.0)
            to_high += jnp.where((lane >= 56) & (lane < 64) & up_g, wide(move(halo_c[2], -8)), 0.0)
        if a == 7:
            to_low += jnp.where((lane >= 192) & (lane < 200) & down_g, wide(move(halo_c[1], 8)), 0.0)
            to_high += jnp.where((lane >= 248) & down_g, wide(move(halo_c[0], 120)), 0.0)
        new_low = jnp.where(ey > 0, move(high, 8), jnp.where(up_d, to_low, 0.0))
        new_high = jnp.where(ey < 7, move(low, -8), jnp.where(down_d, to_high, 0.0))
        planes_now[a, 0] = low + new_low
        planes_now[a, 7] = high + new_high
    for ab in OUTER:
        put(mid, *ab, planes_now[ab])

    await_bytes(c2r.at[1:], c2_rsem)
    total = c2r[0]
    for k in range(1, n_grp * planes):
        total += c2r[k]
    cost[...] = total
    await_bytes(recv.at[1:], send_sem)
    await_bytes(c1r.at[1:], c1_ssem)
    await_bytes(c2r.at[1:], c2_ssem)
    for kind, ref in enumerate((halo_g, halo_d, halo_c)):
        await_bytes(ref, h_ssem.at[kind])


def finish_kernel(mid, cost_row, out, cost):
    shape = (8, 128)
    ez = lanes_of(shape) & 7
    row = rows_of(shape)
    done = {}
    for ab in GROUPS:
        now = mid[PLACE[ab] : PLACE[ab] + 8, :]
        z = jnp.where(row == 7, move(now, 1), move(now, -1))
        to_low = jnp.where((row == 0) & (ez > 0), pltpu.roll(z, 1, 0), 0.0)
        to_high = jnp.where((row == 7) & (ez < 7), pltpu.roll(z, 7, 0), 0.0)
        done[ab] = now + to_low + to_high
    for a in range(0, 8, 2):
        both = jnp.concatenate([done[k, b] for k in (a, a + 1) for b in range(8)], axis=0)
        out[:, 64 * a : 64 * a + 128] = both.T
    cost[0, 0] = 0.5 * jnp.sum(cost_row[...])


def on_device(coord, resid, weight, dest, slot, elem, n_grp, n_dev):
    rows = resid.shape[0] // 128
    flat = [v.reshape(rows, 128) for v in (resid, weight, dest, slot, elem)]
    co = min(COPLANE, n_dev)
    blocks = n_grp * (n_dev // co)
    dma = pltpu.SemaphoreType.DMA
    vmem = pl.BlockSpec(memory_space=pltpu.VMEM)
    mid, cost_row = pl.pallas_call(
        functools.partial(exchange_kernel, n_grp, n_dev),
        out_shape=(
            jax.ShapeDtypeStruct((NODES, ELEM), F32),
            jax.ShapeDtypeStruct((1, 128), F32),
        ),
        in_specs=[pl.BlockSpec(memory_space=pltpu.HBM)] * 6,
        out_specs=(vmem, vmem),
        scratch_shapes=[
            pltpu.VMEM(coord.shape, F32),
            pltpu.VMEM((rows, 128), F32),
            pltpu.VMEM((rows, 128), F32),
            pltpu.VMEM((rows, 128), I32),
            pltpu.VMEM((rows, 128), I32),
            pltpu.VMEM((rows, 128), I32),
            pltpu.VMEM((9 * 32, rows * 128), BF16),
            pltpu.VMEM((256, rows * 128), BF16),
            pltpu.VMEM((PEERS, 5, CAP), F32),
            pltpu.VMEM((n_dev, 5, CAP), F32),
            pltpu.VMEM((2 * SPLIT, n_dev * CAP), BF16),
            pltpu.VMEM((2 * (NODES - SPLIT), n_dev * CAP), BF16),
            pltpu.VMEM((ELEM, n_dev * CAP), BF16),
            pltpu.VMEM((2 * SPLIT, ELEM), F32),
            pltpu.VMEM((SPLIT, ELEM), F32),
            pltpu.VMEM((1, 128), F32),
            pltpu.VMEM((co, 1, 128), F32),
            pltpu.VMEM((1, 128), F32),
            pltpu.VMEM((blocks, 1, 128), F32),
            pltpu.VMEM((2, 64, 128), F32),
            pltpu.VMEM((2, 64, 128), F32),
            pltpu.VMEM((4, 8, 128), F32),
            pltpu.VMEM((2, 64, 128), F32),
            dma((6,)),
            dma,
            dma((4 if n_dev == 64 else 2,)),
            dma,
            dma,
            dma,
            dma,
            dma((3,)),
            dma((3,)),
        ],
        compiler_params=pltpu.CompilerParams(
            collective_id=0, has_side_effects=True, vmem_limit_bytes=48 * 1024 * 1024
        ),
    )(*[pltpu.with_memory_space_constraint(v, pltpu.HBM) for v in (coord, *flat)])
    out, cost = pl.pallas_call(
        finish_kernel,
        grid=(ELEM // 128,),
        out_shape=(
            jax.ShapeDtypeStruct((ELEM, NODES), F32),
            jax.ShapeDtypeStruct((1, 1), F32),
        ),
        in_specs=[
            pl.BlockSpec((NODES, 128), lambda i: (0, i)),
            pl.BlockSpec((1, 128), lambda i: (0, 0)),
        ],
        out_specs=(
            pl.BlockSpec((128, NODES), lambda i: (i, 0)),
            pl.BlockSpec(memory_space=pltpu.SMEM),
        ),
        compiler_params=pltpu.CompilerParams(vmem_limit_bytes=16 * 1024 * 1024),
    )(mid, cost_row)
    return out.reshape(4, 8, 8, NODES), cost.reshape(())


def solution(mesh):
    n_grp, n_dev = mesh.shape["grp"], mesh.shape["dev"]
    rows = P(("grp", "dev"))

    def step(obs_coord, obs_resid, obs_weight, obs_dest, obs_send_slot, obs_elem, obs_slot):
        del obs_slot
        return on_device(
            obs_coord, obs_resid, obs_weight, obs_dest, obs_send_slot, obs_elem, n_grp, n_dev
        )

    return jax.shard_map(
        step,
        mesh=mesh,
        in_specs=(P(None, ("grp", "dev")), rows, rows, rows, rows, rows, rows),
        out_specs=(P("grp", "dev", None, None), P()),
        check_vma=False,
    )
```

time: 40.6 us -> 33.3 us (0.82)
  Pallas kernels: 36.2 us -> 32.4 us
  local copies, waits for them, and re-layouts: 1.87 us -> 0 us
  between operations: 2.34 us -> 0.64 us
    pallas_call x1 -> x2, Pallas kernels: 36.2 us -> 32.4 us  [the longest x1 31 us: on_device(): pl.pallas_call(functools.partial(exchange_kernel, n_grp, n_dev), out_shap...]
    unnamed x1 -> x0, local copies, waits for them, and re-layouts: 1.87 us -> none
where the time goes in v2:
time: 33.3 us; the launch traced here: 33.1 us
  Pallas kernels  32.4 us (97%)
  between operations  0.64 us (2%)
    pallas_call x1, Pallas kernels, on_device(): pl.pallas_call(functools.partial(exchange_kernel, n_grp, n_dev), out_shap...  31 us
    pallas_call x1, Pallas kernels, on_device(): pl.pallas_call(finish_kernel, grid=(ELEM // 128,), out_shape=(jax.ShapeDt...  1.44 us

profile of v2, /device:TPU:1, one launch (start us, length us, event | category | flops | bytes accessed | tf_op | source)
XLA Modules:
  0.0 33.1 jit_solution(8704375976234134648)
XLA Ops:
  0.6 31.0 %shard_map.77 = (f32[512,256]{1,0:T(8,128)S(1)}, f32[1,128]{1,0:T(1,128)S(1)}) custom-call(f32[3,4096]{1,0:T(4,128)} %coord.1, f32[32,128]{1,0:T(8,128)} %bitcast.7, f32[32,128]{1,0:T(8,128)} %bitcast.8, s32[32,128]{1,0:T(8,128)} %bitcast.9, s32[32,128]{1,0:T(8,128)} %bitcast.10, s32[32,128]{1,0:T(8,128)} %bitcast.11), custom_call_target="tpu_custom_call" | custom-call | tf_op jit(solution)/shard_map/pallas_call | solution.py:354
  31.7 1.4 %shard_map.78 = (f32[256,512]{1,0:T(8,128)}, f32[1,1]{1,0:T(1,128)}) custom-call(f32[512,256]{1,0:T(8,128)S(1)} %get-tuple-element.6.mid, f32[1,128]{1,0:T(1,128)S(1)} %get-tuple-element.7.cost_row), custom_call_target="tpu_custom_call" | custom-call | tf_op jit(solution)/shard_map/pallas_call | solution.py:400

commit v3 on v2

--- a/solution.py
+++ b/solution.py
@@ -37,6 +37,10 @@
     return [0] + sorted(range(1, n_dev), key=lambda o: (hops(o), o))
 
 
+def bounds_of(n_dev):
+    return [0, 16, 32, 48, 56, 64] if n_dev == 64 else [0, 2, 4]
+
+
 def lanes_of(shape):
     return lax.broadcasted_iota(I32, shape, len(shape) - 1)
 
@@ -75,7 +79,7 @@
 def exchange_kernel(
     n_grp, n_dev, coord, resid, weight, dest, slot, elem, mid, cost,
     coord_v, resid_v, weight_v, dest_v, slot_v, elem_v,
-    lhs, pick, send, recv, xo, xi, oh, acc, outer,
+    lhs, pick, send, recv, acc, outer, xo, xi, oh,
     c1s, c1r, c2s, c2r, halo_g, halo_d, halo_c, dsend,
     in_sem, send_sem, recv_sem, c1_ssem, c1_rsem, c2_ssem, c2_rsem, h_ssem, h_rsem,
 ):
@@ -139,7 +143,7 @@
 
     pl.semaphore_wait(barrier, len(peers))
 
-    bounds = [0, 24, 44, 56, 64] if n_dev == 64 else [0, 2, 4]
+    bounds = bounds_of(n_dev)
     chunks = list(zip(bounds[:-1], bounds[1:]))
     chunk_of = [i for i, (first, last) in enumerate(chunks) for _ in range(first, last)]
 
@@ -178,52 +182,52 @@
         for k, p in rest
     ]
 
-    def build(p):
+    def build(i, p):
         first, second = recv[2 * p], recv[2 * p + 1]
 
         def row(c):
             return jnp.concatenate([first[c : c + 1], second[c : c + 1]], axis=1)
 
-        cols = slice(256 * p, 256 * p + 256)
+        begin = 256 * p - CAP * chunks[i][0]
+        cols = slice(begin, begin + 256)
         fa = basis(row(0)) * row(3)
         fb = basis(row(1))
         fc = basis(row(2))
-        for i in range(0, 64, 2):
-            full = jnp.concatenate(
-                [fa[a : a + 1] * fb[b : b + 1] * fc for a, b in GROUPS[i : i + 2]], axis=0
-            )
+        bc = [fb[b : b + 1] * fc for b in range(8)]
+        for k in range(0, 64, 2):
+            full = jnp.concatenate([fa[a : a + 1] * bc[b] for a, b in GROUPS[k : k + 2]], axis=0)
             high = full.astype(BF16)
             low = (full - high.astype(F32)).astype(BF16)
-            ref, row_of, count = (xo, 8 * i, SPLIT) if 8 * i < SPLIT else (xi, 8 * i - SPLIT, NODES - SPLIT)
+            ref, row_of, count = (xo[i], 8 * k, SPLIT) if 8 * k < SPLIT else (xi[i], 8 * k - SPLIT, NODES - SPLIT)
             ref[row_of : row_of + 16, cols] = high
             ref[count + row_of : count + row_of + 16, cols] = low
-        oh[:, cols] = one_hot(row(4), ELEM)
-
-    def product(ref, cols):
-        return lax.dot_general(ref[:, cols], oh[:, cols], NT, preferred_element_type=F32)
+        oh[i][:, cols] = one_hot(row(4), ELEM)
+
+    def product(ref, i):
+        return lax.dot_general(ref[i][...], oh[i][...], NT, preferred_element_type=F32)
 
     def arrived(i):
         first, last = max(chunks[i][0], 1), chunks[i][1]
         await_bytes(recv.at[first:last], recv_sem.at[i])
 
-    def cols_of(first, last):
-        return slice(128 * first, 128 * last)
-
-    arrived(0)
-    for p in range(chunks[0][0] // 2, chunks[0][1] // 2):
-        build(p)
-    for i, chunk in enumerate(chunks):
-        if i + 1 < len(chunks):
-            arrived(i + 1)
-        now = product(xo, cols_of(*chunk))
-        if i > 0:
-            now = acc[...] + now
-        if i + 1 < len(chunks):
-            acc[...] = now
-            for p in range(chunks[i + 1][0] // 2, chunks[i + 1][1] // 2):
-                build(p)
-        else:
-            outer[...] = now[:SPLIT] + now[SPLIT:]
+    def block_of(body):
+        pl.when(d >= 0)(body)
+
+    for i in range(len(chunks)):
+        arrived(i)
+
+        @block_of
+        def _():
+            for p in range(chunks[i][0] // 2, chunks[i][1] // 2):
+                build(i, p)
+            now = product(xo, i)
+            if i > 0:
+                now = acc[...] + now
+            if i + 1 < len(chunks):
+                acc[...] = now
+            else:
+                outer[...] = now[:SPLIT] + now[SPLIT:]
+
         if i == 1:
             await_bytes(c1r.at[1:co], c1_rsem)
             total = c1r[0]
@@ -277,8 +281,11 @@
     ]
     for m in halos:
         m.start()
-    left = product(xi, slice(0, n_dev * CAP))
-    mid[SPLIT:, :] = left[: NODES - SPLIT] + left[NODES - SPLIT :]
+    @block_of
+    def _():
+        left = sum(product(xi, i) for i in range(len(chunks)))
+        mid[SPLIT:, :] = left[: NODES - SPLIT] + left[NODES - SPLIT :]
+
 
     for kind, ref in enumerate((halo_g, halo_d, halo_c)):
         await_bytes(ref, h_rsem.at[kind])
@@ -350,6 +357,8 @@
     co = min(COPLANE, n_dev)
     blocks = n_grp * (n_dev // co)
     dma = pltpu.SemaphoreType.DMA
+    bounds = bounds_of(n_dev)
+    widths = [CAP * (last - first) for first, last in zip(bounds[:-1], bounds[1:])]
     vmem = pl.BlockSpec(memory_space=pltpu.VMEM)
     mid, cost_row = pl.pallas_call(
         functools.partial(exchange_kernel, n_grp, n_dev),
@@ -370,11 +379,11 @@
             pltpu.VMEM((256, rows * 128), BF16),
             pltpu.VMEM((PEERS, 5, CAP), F32),
             pltpu.VMEM((n_dev, 5, CAP), F32),
-            pltpu.VMEM((2 * SPLIT, n_dev * CAP), BF16),
-            pltpu.VMEM((2 * (NODES - SPLIT), n_dev * CAP), BF16),
-            pltpu.VMEM((ELEM, n_dev * CAP), BF16),
             pltpu.VMEM((2 * SPLIT, ELEM), F32),
             pltpu.VMEM((SPLIT, ELEM), F32),
+            [pltpu.VMEM((2 * SPLIT, n), BF16) for n in widths],
+            [pltpu.VMEM((2 * (NODES - SPLIT), n), BF16) for n in widths],
+            [pltpu.VMEM((ELEM, n), BF16) for n in widths],
             pltpu.VMEM((1, 128), F32),
             pltpu.VMEM((co, 1, 128), F32),
             pltpu.VMEM((1, 128), F32),
@@ -385,7 +394,7 @@
             pltpu.VMEM((2, 64, 128), F32),
             dma((6,)),
             dma,
-            dma((4 if n_dev == 64 else 2,)),
+            dma((len(widths),)),
             dma,
             dma,
             dma,

time: 33.3 us -> 28.3 us (0.85)
  Pallas kernels: 32.4 us -> 27.5 us
    pallas_call x1, Pallas kernels: 31 us -> 26.1 us  [on_device(): pl.pallas_call(functools.partial(exchange_kernel, n_grp, n_dev), out_shap...]
where the time goes in v3:
time: 28.3 us; the launch traced here: 28.2 us
  Pallas kernels  27.5 us (97%)
  between operations  0.64 us (2%)
    pallas_call x1, Pallas kernels, on_device(): pl.pallas_call(functools.partial(exchange_kernel, n_grp, n_dev), out_shap...  26.1 us
    pallas_call x1, Pallas kernels, on_device(): pl.pallas_call(finish_kernel, grid=(ELEM // 128,), out_shape=(jax.ShapeDt...  1.44 us

profile of v3, /device:TPU:1, one launch (start us, length us, event | category | flops | bytes accessed | tf_op | source)
XLA Modules:
  0.0 28.2 jit_solution(9811573698609177399)
XLA Ops:
  0.6 26.1 %shard_map.77 = (f32[512,256]{1,0:T(8,128)S(1)}, f32[1,128]{1,0:T(1,128)S(1)}) custom-call(f32[3,4096]{1,0:T(4,128)} %coord.1, f32[32,128]{1,0:T(8,128)} %bitcast.7, f32[32,128]{1,0:T(8,128)} %bitcast.8, s32[32,128]{1,0:T(8,128)} %bitcast.9, s32[32,128]{1,0:T(8,128)} %bitcast.10, s32[32,128]{1,0:T(8,128)} %bitcast.11), custom_call_target="tpu_custom_call" | custom-call | tf_op jit(solution)/shard_map/pallas_call | solution.py:363
  26.7 1.4 %shard_map.78 = (f32[256,512]{1,0:T(8,128)}, f32[1,1]{1,0:T(1,128)}) custom-call(f32[512,256]{1,0:T(8,128)S(1)} %get-tuple-element.6.mid, f32[1,128]{1,0:T(1,128)S(1)} %get-tuple-element.7.cost_row), custom_call_target="tpu_custom_call" | custom-call | tf_op jit(solution)/shard_map/pallas_call | solution.py:409

commit v4 on v3

--- a/solution.py
+++ b/solution.py
@@ -38,7 +38,7 @@
 
 
 def bounds_of(n_dev):
-    return [0, 16, 32, 48, 56, 64] if n_dev == 64 else [0, 2, 4]
+    return [0, 16, 32, 48, 60, 64] if n_dev == 64 else [0, 2, 4]
 
 
 def lanes_of(shape):
@@ -79,8 +79,8 @@
 def exchange_kernel(
     n_grp, n_dev, coord, resid, weight, dest, slot, elem, mid, cost,
     coord_v, resid_v, weight_v, dest_v, slot_v, elem_v,
-    lhs, pick, send, recv, acc, outer, xo, xi, oh,
-    c1s, c1r, c2s, c2r, halo_g, halo_d, halo_c, dsend,
+    lhs, pick, send, recv, acc, outer, summed, bases, xo, xi, oh,
+    c1s, c1r, c2s, c2r, halo_g, halo_d, halo_c, gsend, dsend,
     in_sem, send_sem, recv_sem, c1_ssem, c1_rsem, c2_ssem, c2_rsem, h_ssem, h_rsem,
 ):
     g, d = lax.axis_index("grp"), lax.axis_index("dev")
@@ -99,15 +99,15 @@
             [(dest, dest_v), (slot, slot_v), (elem, elem_v), (coord, coord_v), (resid, resid_v), (weight, weight_v)]
         )
     ]
-    for load in loads:
-        load.start()
-
     barrier = pltpu.get_barrier_semaphore()
     corners = [(-1, -1), (-1, 1), (1, -1), (1, 1)]
     peers = [(k, p * co) for k in range(1, n_grp) for p in range(planes)]
     peers += corners
     peers += [(0, o) for o in order[1:]]
-    for dg, dd in reversed(peers):
+    for i, (dg, dd) in enumerate(reversed(peers)):
+        if i == len(peers) // 2:
+            for load in loads:
+                load.start()
         pl.semaphore_signal(barrier, inc=1, device_id=at(dg, dd))
     for load in loads:
         load.wait()
@@ -160,9 +160,6 @@
     def await_bytes(ref, sem):
         pltpu.make_async_copy(ref, ref, sem).wait()
 
-    for k in range(1, n_dev):
-        message(k).start()
-
     def partial_one(k):
         return pltpu.make_async_remote_copy(
             src_ref=c1s, dst_ref=c1r.at[here], send_sem=c1_ssem, recv_sem=c1_rsem,
@@ -171,6 +168,8 @@
 
     for k in range(1, co):
         partial_one(k).start()
+    for k in range(1, n_dev):
+        message(k).start()
 
     mine = g * planes + block // co
     rest = [(k, p) for k in range(n_grp) for p in range(planes) if k or p]
@@ -182,25 +181,33 @@
         for k, p in rest
     ]
 
+    def rows_built(ref, cols, groups, fa, fb, fc):
+        bc = [fb[b : b + 1] * fc for b in range(8)]
+        count = 8 * len(groups)
+        for k in range(0, len(groups), 2):
+            full = jnp.concatenate([fa[a : a + 1] * bc[b] for a, b in groups[k : k + 2]], axis=0)
+            high = full.astype(BF16)
+            low = (full - high.astype(F32)).astype(BF16)
+            ref[8 * k : 8 * k + 16, cols] = high
+            ref[count + 8 * k : count + 8 * k + 16, cols] = low
+
+    def cols_of(i, p):
+        begin = 256 * p - CAP * chunks[i][0]
+        return slice(begin, begin + 256)
+
     def build(i, p):
         first, second = recv[2 * p], recv[2 * p + 1]
 
         def row(c):
             return jnp.concatenate([first[c : c + 1], second[c : c + 1]], axis=1)
 
-        begin = 256 * p - CAP * chunks[i][0]
-        cols = slice(begin, begin + 256)
+        cols = cols_of(i, p)
         fa = basis(row(0)) * row(3)
         fb = basis(row(1))
         fc = basis(row(2))
-        bc = [fb[b : b + 1] * fc for b in range(8)]
-        for k in range(0, 64, 2):
-            full = jnp.concatenate([fa[a : a + 1] * bc[b] for a, b in GROUPS[k : k + 2]], axis=0)
-            high = full.astype(BF16)
-            low = (full - high.astype(F32)).astype(BF16)
-            ref, row_of, count = (xo[i], 8 * k, SPLIT) if 8 * k < SPLIT else (xi[i], 8 * k - SPLIT, NODES - SPLIT)
-            ref[row_of : row_of + 16, cols] = high
-            ref[count + row_of : count + row_of + 16, cols] = low
+        for c, value in enumerate((fa, fb, fc)):
+            bases[c, p] = value
+        rows_built(xo[i], cols, OUTER, fa, fb, fc)
         oh[i][:, cols] = one_hot(row(4), ELEM)
 
     def product(ref, i):
@@ -238,52 +245,66 @@
             for m in twos:
                 m.start()
 
-    lane = lanes_of((8, ELEM))
-
-    def rg(ref, a, b):
-        return ref[PLACE[a, b] : PLACE[a, b] + 8, :]
-
-    def put(ref, a, b, value):
-        ref[PLACE[a, b] : PLACE[a, b] + 8, :] = value
-
-    for b in range(8):
-        low, high = rg(outer, 0, b), rg(outer, 7, b)
-        put(outer, 0, b, low + jnp.where(lane >= 64, move(high, 64), 0.0))
-        put(outer, 7, b, high + jnp.where(lane < 192, move(low, -64), 0.0))
-    half = lanes_of((8, 128))
-    for a in range(8):
-        for side, b in ((0, 0), (1, 7)):
-            plane = rg(outer, a, b)
-            near = ((half >> 3) & 7) == b
-            left = jnp.where(near, plane[:, :128], 0.0)
-            right = jnp.where(near, plane[:, 128:], 0.0)
-            dsend[side, 8 * a : 8 * a + 8, :] = left + move(right, 8 if b == 0 else -8)
-
     def halo(kind, src, dst, dg, dd):
         return pltpu.make_async_remote_copy(
             src_ref=src, dst_ref=dst, send_sem=h_ssem.at[kind], recv_sem=h_rsem.at[kind],
             device_id=at(dg, dd),
         )
 
-    def tile(a, b, count, right):
-        first = PLACE[a, b]
-        return outer.at[first : first + 8 * count, (128 if right else 0) : (256 if right else 128)]
-
-    halos = [
-        halo(0, tile(0, 0, 8, False), halo_g.at[0], -1, 0),
-        halo(0, tile(7, 0, 8, True), halo_g.at[1], 1, 0),
-        halo(1, dsend.at[0], halo_d.at[0], 0, -1),
-        halo(1, dsend.at[1], halo_d.at[1], 0, 1),
-        halo(2, tile(0, 0, 1, False), halo_c.at[0], -1, -1),
-        halo(2, tile(0, 7, 1, False), halo_c.at[1], -1, 1),
-        halo(2, tile(7, 0, 1, True), halo_c.at[2], 1, -1),
-        halo(2, tile(7, 7, 1, True), halo_c.at[3], 1, 1),
-    ]
-    for m in halos:
-        m.start()
+    def line(a, b):
+        first, half = PLACE[a, b], 128 if a else 0
+        return outer.at[first : first + 8, half : half + 128]
+
+    for i, (dg, dd) in enumerate(corners):
+        halo(2, line(0 if dg < 0 else 7, 0 if dd < 0 else 7), halo_c.at[i], dg, dd).start()
+
+    lane = lanes_of((8, ELEM))
+    half = lanes_of((8, 128))
+
+    def rg(ref, a, b):
+        return ref[PLACE[a, b] : PLACE[a, b] + 8, :]
+
+    def put(ref, a, b, value):
+        ref[PLACE[a, b] : PLACE[a, b] + 8, :] = value
+
+    now = {ab: rg(outer, *ab) for ab in OUTER}
+    for b in (0, 7, 1, 2, 3, 4, 5, 6):
+        low, high = now[0, b], now[7, b]
+        now[0, b] = low + jnp.where(lane >= 64, move(high, 64), 0.0)
+        now[7, b] = high + jnp.where(lane < 192, move(low, -64), 0.0)
+        put(summed, 0, b, now[0, b])
+        put(summed, 7, b, now[7, b])
+    for side, b, step in ((0, 0, 8), (1, 7, -8)):
+        near = ((half >> 3) & 7) == b
+        for first in (0, 4):
+            packed_planes = None
+            for j in range(4):
+                plane = now[first + j, b]
+                left = jnp.where(near, plane[:, :128], 0.0)
+                right = jnp.where(near, plane[:, 128:], 0.0)
+                piece = move(left + move(right, step), 2 * step * j)
+                packed_planes = piece if j == 0 else packed_planes + piece
+            dsend[side, 2 * first : 2 * first + 8, :] = packed_planes
+    for side, dd in enumerate((-1, 1)):
+        halo(1, dsend.at[side], halo_d.at[side], 0, dd).start()
+    for b in range(4):
+        gsend[0, 8 * b : 8 * b + 8, :] = jnp.where(
+            half < 64, rg(outer, 0, b)[:, :128], move(rg(outer, 0, b + 4)[:, :128], 64)
+        )
+        gsend[1, 8 * b : 8 * b + 8, :] = jnp.where(
+            half < 64, move(rg(outer, 7, b)[:, 128:], 64), rg(outer, 7, b + 4)[:, 128:]
+        )
+    for side, dg in enumerate((-1, 1)):
+        halo(0, gsend.at[side], halo_g.at[side], dg, 0).start()
+
     @block_of
     def _():
-        left = sum(product(xi, i) for i in range(len(chunks)))
+        left = None
+        for i, (first, last) in enumerate(chunks):
+            for p in range(first // 2, last // 2):
+                rows_built(xi[i], cols_of(i, p), INNER, *[bases[c, p] for c in range(3)])
+            now = product(xi, i)
+            left = now if left is None else left + now
         mid[SPLIT:, :] = left[: NODES - SPLIT] + left[NODES - SPLIT :]
 
 
@@ -297,18 +318,23 @@
     def wide(value):
         return jnp.concatenate([value, value], axis=1)
 
-    planes_now = {ab: rg(outer, *ab) for ab in OUTER}
+    planes_now = {(a, b): rg(summed if a in EDGE else outer, a, b) for a, b in OUTER}
     for b in range(8):
-        from_low = move(halo_g[1, 8 * b : 8 * b + 8, :], 64)
-        from_high = move(halo_g[0, 8 * b : 8 * b + 8, :], 64)
+        part = slice(8 * (b % 4), 8 * (b % 4) + 8)
+        from_low, from_high = halo_g[1, part, :], halo_g[0, part, :]
+        if b < 4:
+            from_high = move(from_high, 64)
+        else:
+            from_low = move(from_low, 64)
         planes_now[0, b] += jnp.where((lane < 64) & up_g, wide(from_low), 0.0)
         planes_now[7, b] += jnp.where((lane >= 192) & down_g, wide(from_high), 0.0)
     for a in range(8):
         low, high = planes_now[a, 0], planes_now[a, 7]
-        theirs = halo_d[1, 8 * a : 8 * a + 8, :]
-        to_low = jnp.concatenate([move(theirs, -56), move(theirs, -48)], axis=1)
-        theirs = halo_d[0, 8 * a : 8 * a + 8, :]
-        to_high = jnp.concatenate([move(theirs, 56), move(theirs, 48)], axis=1)
+        part, shift = slice(8 * (a // 4), 8 * (a // 4) + 8), 16 * (a % 4)
+        theirs = halo_d[1, part, :]
+        to_low = jnp.concatenate([move(theirs, shift - 56), move(theirs, shift - 48)], axis=1)
+        theirs = halo_d[0, part, :]
+        to_high = jnp.concatenate([move(theirs, 56 - shift), move(theirs, 48 - shift)], axis=1)
         if a == 0:
             to_low += jnp.where((lane < 8) & up_g, wide(move(halo_c[3], -120)), 0.0)
             to_high += jnp.where((lane >= 56) & (lane < 64) & up_g, wide(move(halo_c[2], -8)), 0.0)
@@ -381,6 +407,8 @@
             pltpu.VMEM((n_dev, 5, CAP), F32),
             pltpu.VMEM((2 * SPLIT, ELEM), F32),
             pltpu.VMEM((SPLIT, ELEM), F32),
+            pltpu.VMEM((128, ELEM), F32),
+            pltpu.VMEM((3, n_dev // 2, 8, 256), F32),
             [pltpu.VMEM((2 * SPLIT, n), BF16) for n in widths],
             [pltpu.VMEM((2 * (NODES - SPLIT), n), BF16) for n in widths],
             [pltpu.VMEM((ELEM, n), BF16) for n in widths],
@@ -388,10 +416,11 @@
             pltpu.VMEM((co, 1, 128), F32),
             pltpu.VMEM((1, 128), F32),
             pltpu.VMEM((blocks, 1, 128), F32),
-            pltpu.VMEM((2, 64, 128), F32),
-            pltpu.VMEM((2, 64, 128), F32),
+            pltpu.VMEM((2, 32, 128), F32),
+            pltpu.VMEM((2, 16, 128), F32),
             pltpu.VMEM((4, 8, 128), F32),
-            pltpu.VMEM((2, 64, 128), F32),
+            pltpu.VMEM((2, 32, 128), F32),
+            pltpu.VMEM((2, 16, 128), F32),
             dma((6,)),
             dma,
             dma((len(widths),)),

time: 28.3 us -> 26.6 us (0.940)
  Pallas kernels: 27.5 us -> 25.8 us
    pallas_call x1, Pallas kernels: 26.1 us -> 24.3 us  [on_device(): pl.pallas_call(functools.partial(exchange_kernel, n_grp, n_dev), out_shap...]
where the time goes in v4:
time: 26.6 us; the launch traced here: 26.4 us
  Pallas kernels  25.8 us (97%)
  between operations  0.64 us (2%)
    pallas_call x1, Pallas kernels, on_device(): pl.pallas_call(functools.partial(exchange_kernel, n_grp, n_dev), out_shap...  24.3 us
    pallas_call x1, Pallas kernels, on_device(): pl.pallas_call(finish_kernel, grid=(ELEM // 128,), out_shape=(jax.ShapeDt...  1.44 us

profile of v4, /device:TPU:1, one launch (start us, length us, event | category | flops | bytes accessed | tf_op | source)
XLA Modules:
  0.0 26.4 jit_solution(16785266462449662658)
XLA Ops:
  0.6 24.3 %shard_map.77 = (f32[512,256]{1,0:T(8,128)S(1)}, f32[1,128]{1,0:T(1,128)S(1)}) custom-call(f32[3,4096]{1,0:T(4,128)} %coord.1, f32[32,128]{1,0:T(8,128)} %bitcast.7, f32[32,128]{1,0:T(8,128)} %bitcast.8, s32[32,128]{1,0:T(8,128)} %bitcast.9, s32[32,128]{1,0:T(8,128)} %bitcast.10, s32[32,128]{1,0:T(8,128)} %bitcast.11), custom_call_target="tpu_custom_call" | custom-call | tf_op jit(solution)/shard_map/pallas_call | solution.py:389
  25.0 1.4 %shard_map.78 = (f32[256,512]{1,0:T(8,128)}, f32[1,1]{1,0:T(1,128)}) custom-call(f32[512,256]{1,0:T(8,128)S(1)} %get-tuple-element.6.mid, f32[1,128]{1,0:T(1,128)S(1)} %get-tuple-element.7.cost_row), custom_call_target="tpu_custom_call" | custom-call | tf_op jit(solution)/shard_map/pallas_call | solution.py:438

commit v5 on v4

--- a/solution.py
+++ b/solution.py
@@ -29,16 +29,19 @@
 SPLIT = 8 * len(OUTER)
 
 
-def peer_order(n_dev):
-    def hops(offset):
-        y, z = offset // COPLANE, (offset % COPLANE) // 2
-        return min(y, max(n_dev // COPLANE, 1) - y) + min(z, COPLANE // 2 - z)
-
-    return [0] + sorted(range(1, n_dev), key=lambda o: (hops(o), o))
+def peer_steps(n_dev):
+    size_y, size_z = n_dev // min(COPLANE, n_dev), min(COPLANE, n_dev) // 2
+    steps = [(y, z, c) for y in range(size_y) for z in range(size_z) for c in range(2)]
+
+    def hops(step):
+        y, z, _ = step
+        return min(y, size_y - y) + min(z, size_z - z)
+
+    return sorted(steps, key=lambda step: (hops(step), step))
 
 
 def bounds_of(n_dev):
-    return [0, 16, 32, 48, 60, 64] if n_dev == 64 else [0, 2, 4]
+    return [0, 8, 24, 40, 52, 64] if n_dev == 64 else [0, 2, 4]
 
 
 def lanes_of(shape):
@@ -64,10 +67,17 @@
 def basis(t):
     shape = (8, t.shape[1])
     t = jnp.broadcast_to(t, shape)
+    square = t * t
     row = rows_of(shape)
+    pair = jnp.minimum(row, 7 - row)
+    point, scale = F32(NODE_POINTS[7]), F32(NODE_SCALE[7])
+    for a in range(7):
+        point = jnp.where(row == a, F32(NODE_POINTS[a]), point)
+        scale = jnp.where(row == a, F32(NODE_SCALE[a]), scale)
+    own = (t + point) * scale
     out = None
-    for m in range(8):
-        factor = jnp.where(row == m, F32(NODE_SCALE[m]), t - F32(NODE_POINTS[m]))
+    for m in range(4):
+        factor = jnp.where(pair == m, own, square - F32(NODE_POINTS[m] ** 2))
         out = factor if out is None else out * factor
     return out
 
@@ -86,9 +96,14 @@
     g, d = lax.axis_index("grp"), lax.axis_index("dev")
     co = min(COPLANE, n_dev)
     planes = n_dev // co
-    order = peer_order(n_dev)
+    steps = peer_steps(n_dev)
     here = lax.rem(d, co)
     block = d - here
+    y, z, core = d // co, here // 2, lax.rem(d, 2)
+    to_y = [lax.rem(y + k, planes) * co for k in range(planes)]
+    to_z = [lax.rem(z + k, co // 2) * 2 for k in range(co // 2)]
+    to_core = [core, 1 - core]
+    peer_at = [to_y[i] + to_z[j] + to_core[k] for i, j, k in steps]
 
     def at(dg, dd):
         return {"grp": lax.rem(g + dg + n_grp, n_grp), "dev": lax.rem(d + dd + n_dev, n_dev)}
@@ -103,12 +118,13 @@
     corners = [(-1, -1), (-1, 1), (1, -1), (1, 1)]
     peers = [(k, p * co) for k in range(1, n_grp) for p in range(planes)]
     peers += corners
-    peers += [(0, o) for o in order[1:]]
-    for i, (dg, dd) in enumerate(reversed(peers)):
-        if i == len(peers) // 2:
+    targets = [{"grp": g, "dev": peer} for peer in reversed(peer_at[1:])]
+    targets += [at(dg, dd) for dg, dd in peers]
+    for i, target in enumerate(targets):
+        if i == len(targets) // 2:
             for load in loads:
                 load.start()
-        pl.semaphore_signal(barrier, inc=1, device_id=at(dg, dd))
+        pl.semaphore_signal(barrier, inc=1, device_id=target)
     for load in loads:
         load.wait()
 
@@ -141,14 +157,14 @@
     recv[0] = send[d]
     c1r[here] = c1s[...]
 
-    pl.semaphore_wait(barrier, len(peers))
+    pl.semaphore_wait(barrier, len(targets))
 
     bounds = bounds_of(n_dev)
     chunks = list(zip(bounds[:-1], bounds[1:]))
     chunk_of = [i for i, (first, last) in enumerate(chunks) for _ in range(first, last)]
 
     def message(k):
-        to = lax.rem(d + order[k], n_dev)
+        to = peer_at[k]
         return pltpu.make_async_remote_copy(
             src_ref=send.at[to],
             dst_ref=recv.at[k],
@@ -245,18 +261,29 @@
             for m in twos:
                 m.start()
 
-    def halo(kind, src, dst, dg, dd):
-        return pltpu.make_async_remote_copy(
-            src_ref=src, dst_ref=dst, send_sem=h_ssem.at[kind], recv_sem=h_rsem.at[kind],
-            device_id=at(dg, dd),
-        )
+    def exists(dg, dd):
+        return (g + dg >= 0) & (g + dg < n_grp) & (d + dd >= 0) & (d + dd < n_dev)
+
+    halo_steps = [(-1, 0), (1, 0), (0, -1), (0, 1)] + corners
+    halo_slots = [halo_g.at[0], halo_g.at[1], halo_d.at[0], halo_d.at[1]]
+    halo_slots += [halo_c.at[i] for i in range(4)]
+
+    def halo(i, src):
+        dg, dd = halo_steps[i]
+
+        @pl.when(exists(dg, dd))
+        def _():
+            pltpu.make_async_remote_copy(
+                src_ref=src, dst_ref=halo_slots[i], send_sem=h_ssem.at[i], recv_sem=h_rsem.at[i],
+                device_id=at(dg, dd),
+            ).start()
 
     def line(a, b):
         first, half = PLACE[a, b], 128 if a else 0
         return outer.at[first : first + 8, half : half + 128]
 
     for i, (dg, dd) in enumerate(corners):
-        halo(2, line(0 if dg < 0 else 7, 0 if dd < 0 else 7), halo_c.at[i], dg, dd).start()
+        halo(4 + i, line(0 if dg < 0 else 7, 0 if dd < 0 else 7))
 
     lane = lanes_of((8, ELEM))
     half = lanes_of((8, 128))
@@ -285,8 +312,8 @@
                 piece = move(left + move(right, step), 2 * step * j)
                 packed_planes = piece if j == 0 else packed_planes + piece
             dsend[side, 2 * first : 2 * first + 8, :] = packed_planes
-    for side, dd in enumerate((-1, 1)):
-        halo(1, dsend.at[side], halo_d.at[side], 0, dd).start()
+    for side in range(2):
+        halo(2 + side, dsend.at[side])
     for b in range(4):
         gsend[0, 8 * b : 8 * b + 8, :] = jnp.where(
             half < 64, rg(outer, 0, b)[:, :128], move(rg(outer, 0, b + 4)[:, :128], 64)
@@ -294,8 +321,8 @@
         gsend[1, 8 * b : 8 * b + 8, :] = jnp.where(
             half < 64, move(rg(outer, 7, b)[:, 128:], 64), rg(outer, 7, b + 4)[:, 128:]
         )
-    for side, dg in enumerate((-1, 1)):
-        halo(0, gsend.at[side], halo_g.at[side], dg, 0).start()
+    for side in range(2):
+        halo(side, gsend.at[side])
 
     @block_of
     def _():
@@ -308,8 +335,12 @@
         mid[SPLIT:, :] = left[: NODES - SPLIT] + left[NODES - SPLIT :]
 
 
-    for kind, ref in enumerate((halo_g, halo_d, halo_c)):
-        await_bytes(ref, h_rsem.at[kind])
+    for i, (dg, dd) in enumerate(halo_steps):
+
+        @pl.when(exists(-dg, -dd))
+        def _():
+            await_bytes(halo_slots[i], h_rsem.at[i])
+
 
     up_g, down_g = g > 0, g < n_grp - 1
     up_d, down_d = d > 0, d < n_dev - 1
@@ -356,8 +387,11 @@
     await_bytes(recv.at[1:], send_sem)
     await_bytes(c1r.at[1:], c1_ssem)
     await_bytes(c2r.at[1:], c2_ssem)
-    for kind, ref in enumerate((halo_g, halo_d, halo_c)):
-        await_bytes(ref, h_ssem.at[kind])
+    for i, (dg, dd) in enumerate(halo_steps):
+
+        @pl.when(exists(dg, dd))
+        def _():
+            await_bytes(halo_slots[i], h_ssem.at[i])
 
 
 def finish_kernel(mid, cost_row, out, cost):
@@ -428,8 +462,8 @@
             dma,
             dma,
             dma,
-            dma((3,)),
-            dma((3,)),
+            dma((8,)),
+            dma((8,)),
         ],
         compiler_params=pltpu.CompilerParams(
             collective_id=0, has_side_effects=True, vmem_limit_bytes=48 * 1024 * 1024

time: 26.6 us -> 25.5 us (0.959)
  Pallas kernels: 25.8 us -> 24.7 us
    pallas_call x1, Pallas kernels: 24.3 us -> 23.3 us  [on_device(): pl.pallas_call(functools.partial(exchange_kernel, n_grp, n_dev), out_shap...]
where the time goes in v5:
time: 25.5 us; the launch traced here: 25.4 us
  Pallas kernels  24.7 us (97%)
  between operations  0.64 us (3%)
    pallas_call x1, Pallas kernels, on_device(): pl.pallas_call(functools.partial(exchange_kernel, n_grp, n_dev), out_shap...  23.3 us
    pallas_call x1, Pallas kernels, on_device(): pl.pallas_call(finish_kernel, grid=(ELEM // 128,), out_shape=(jax.ShapeDt...  1.44 us

profile of v5, /device:TPU:1, one launch (start us, length us, event | category | flops | bytes accessed | tf_op | source)
XLA Modules:
  0.0 25.4 jit_solution(6377072781006366012)
XLA Ops:
  0.6 23.3 %shard_map.77 = (f32[512,256]{1,0:T(8,128)S(1)}, f32[1,128]{1,0:T(1,128)S(1)}) custom-call(f32[3,4096]{1,0:T(4,128)} %coord.1, f32[32,128]{1,0:T(8,128)} %bitcast.7, f32[32,128]{1,0:T(8,128)} %bitcast.8, s32[32,128]{1,0:T(8,128)} %bitcast.9, s32[32,128]{1,0:T(8,128)} %bitcast.10, s32[32,128]{1,0:T(8,128)} %bitcast.11), custom_call_target="tpu_custom_call" | custom-call | tf_op jit(solution)/shard_map/pallas_call | solution.py:423
  23.9 1.4 %shard_map.78 = (f32[256,512]{1,0:T(8,128)}, f32[1,1]{1,0:T(1,128)}) custom-call(f32[512,256]{1,0:T(8,128)S(1)} %get-tuple-element.6.mid, f32[1,128]{1,0:T(1,128)S(1)} %get-tuple-element.7.cost_row), custom_call_target="tpu_custom_call" | custom-call | tf_op jit(solution)/shard_map/pallas_call | solution.py:472

commit v6 on v5

--- a/solution.py
+++ b/solution.py
@@ -182,10 +182,11 @@
             device_id={"grp": g, "dev": block + lax.rem(here + k, co)},
         )
 
-    for k in range(1, co):
-        partial_one(k).start()
     for k in range(1, n_dev):
         message(k).start()
+        if k == n_dev // 4:
+            for j in range(1, co):
+                partial_one(j).start()
 
     mine = g * planes + block // co
     rest = [(k, p) for k in range(n_grp) for p in range(planes) if k or p]
@@ -239,8 +240,7 @@
     for i in range(len(chunks)):
         arrived(i)
 
-        @block_of
-        def _():
+        def contract():
             for p in range(chunks[i][0] // 2, chunks[i][1] // 2):
                 build(i, p)
             now = product(xo, i)
@@ -250,6 +250,11 @@
                 acc[...] = now
             else:
                 outer[...] = now[:SPLIT] + now[SPLIT:]
+
+        if i + 1 < len(chunks):
+            block_of(contract)
+        else:
+            contract()
 
         if i == 1:
             await_bytes(c1r.at[1:co], c1_rsem)

time: 25.5 us -> 25.5 us (level)
  no operation moved by 1% of the time
where the time goes in v6:
time: 25.5 us; the launch traced here: 25.4 us
  Pallas kernels  24.7 us (97%)
  between operations  0.64 us (3%)
    pallas_call x1, Pallas kernels, on_device(): pl.pallas_call(functools.partial(exchange_kernel, n_grp, n_dev), out_shap...  23.3 us
    pallas_call x1, Pallas kernels, on_device(): pl.pallas_call(finish_kernel, grid=(ELEM // 128,), out_shape=(jax.ShapeDt...  1.44 us

profile of v6, /device:TPU:1, one launch (start us, length us, event | category | flops | bytes accessed | tf_op | source)
XLA Modules:
  0.0 25.4 jit_solution(1927037796659838964)
XLA Ops:
  0.6 23.3 %shard_map.77 = (f32[512,256]{1,0:T(8,128)S(1)}, f32[1,128]{1,0:T(1,128)S(1)}) custom-call(f32[3,4096]{1,0:T(4,128)} %coord.1, f32[32,128]{1,0:T(8,128)} %bitcast.7, f32[32,128]{1,0:T(8,128)} %bitcast.8, s32[32,128]{1,0:T(8,128)} %bitcast.9, s32[32,128]{1,0:T(8,128)} %bitcast.10, s32[32,128]{1,0:T(8,128)} %bitcast.11), custom_call_target="tpu_custom_call" | custom-call | tf_op jit(solution)/shard_map/pallas_call | solution.py:428
  23.9 1.4 %shard_map.78 = (f32[256,512]{1,0:T(8,128)}, f32[1,1]{1,0:T(1,128)}) custom-call(f32[512,256]{1,0:T(8,128)S(1)} %get-tuple-element.6.mid, f32[1,128]{1,0:T(1,128)S(1)} %get-tuple-element.7.cost_row), custom_call_target="tpu_custom_call" | custom-call | tf_op jit(solution)/shard_map/pallas_call | solution.py:477

commit v7 on v6

--- a/solution.py
+++ b/solution.py
@@ -237,6 +237,15 @@
     def block_of(body):
         pl.when(d >= 0)(body)
 
+    def inner_rows(which, total):
+        left = None
+        for i in which:
+            for p in range(chunks[i][0] // 2, chunks[i][1] // 2):
+                rows_built(xi[i], cols_of(i, p), INNER, *[bases[c, p] for c in range(3)])
+            now = product(xi, i)
+            left = now if left is None else left + now
+        mid[SPLIT:, :] = total + left[: NODES - SPLIT] + left[NODES - SPLIT :]
+
     for i in range(len(chunks)):
         arrived(i)
 
@@ -256,6 +265,8 @@
         else:
             contract()
 
+        if i == 0:
+            block_of(lambda: inner_rows([0], 0.0))
         if i == 1:
             await_bytes(c1r.at[1:co], c1_rsem)
             total = c1r[0]
@@ -331,13 +342,7 @@
 
     @block_of
     def _():
-        left = None
-        for i, (first, last) in enumerate(chunks):
-            for p in range(first // 2, last // 2):
-                rows_built(xi[i], cols_of(i, p), INNER, *[bases[c, p] for c in range(3)])
-            now = product(xi, i)
-            left = now if left is None else left + now
-        mid[SPLIT:, :] = left[: NODES - SPLIT] + left[NODES - SPLIT :]
+        inner_rows(range(1, len(chunks)), mid[SPLIT:, :])
 
 
     for i, (dg, dd) in enumerate(halo_steps):

time: 25.5 us -> 25.5 us (level)
  no operation moved by 1% of the time
where the time goes in v7:
time: 25.5 us; the launch traced here: 25.4 us
  Pallas kernels  24.7 us (97%)
  between operations  0.64 us (3%)
    pallas_call x1, Pallas kernels, on_device(): pl.pallas_call(functools.partial(exchange_kernel, n_grp, n_dev), out_shap...  23.3 us
    pallas_call x1, Pallas kernels, on_device(): pl.pallas_call(finish_kernel, grid=(ELEM // 128,), out_shape=(jax.ShapeDt...  1.44 us

profile of v7, /device:TPU:1, one launch (start us, length us, event | category | flops | bytes accessed | tf_op | source)
XLA Modules:
  0.0 25.4 jit_solution(4544553403047095758)
XLA Ops:
  0.6 23.3 %shard_map.77 = (f32[512,256]{1,0:T(8,128)S(1)}, f32[1,128]{1,0:T(1,128)S(1)}) custom-call(f32[3,4096]{1,0:T(4,128)} %coord.1, f32[32,128]{1,0:T(8,128)} %bitcast.7, f32[32,128]{1,0:T(8,128)} %bitcast.8, s32[32,128]{1,0:T(8,128)} %bitcast.9, s32[32,128]{1,0:T(8,128)} %bitcast.10, s32[32,128]{1,0:T(8,128)} %bitcast.11), custom_call_target="tpu_custom_call" | custom-call | tf_op jit(solution)/shard_map/pallas_call | solution.py:433
  23.9 1.4 %shard_map.78 = (f32[256,512]{1,0:T(8,128)}, f32[1,1]{1,0:T(1,128)}) custom-call(f32[512,256]{1,0:T(8,128)S(1)} %get-tuple-element.6.mid, f32[1,128]{1,0:T(1,128)S(1)} %get-tuple-element.7.cost_row), custom_call_target="tpu_custom_call" | custom-call | tf_op jit(solution)/shard_map/pallas_call | solution.py:482
